TPU v7x, 512 devices: a 4x2x32 block of a 4x8x32 slice. The times are simulated.
512 devices in a mesh: win: 2 (over y), dx: 32 (over z), dy: 4 (over x), dz: 2 (over core).
Axes of the slice: x: 4, y: 2, z: 32, core: 2. Of those that a mesh axis runs over, the one named last changes fastest.
The devices are a block of a 4x8x32 slice.
Arguments:
- fraction: float32 [3, 64, 4, 2, 768], P(None, ('win', 'dx'), 'dy', 'dz'), parts along dimension 1, may hold values from 0 to 1
- atom_type: int32 [64, 4, 2, 768], P(('win', 'dx'), 'dy', 'dz'), parts along dimension 0, may hold values from 0 to 31
- perturbed: int32 [64, 4, 2, 768], P(('win', 'dx'), 'dy', 'dz'), parts along dimension 0, may hold values from 0 to 1
- leaving: int32 [64, 4, 2, 2, 16], P(('win', 'dx'), 'dy', 'dz'), parts along dimension 0, may hold values from 0 to 767, as said below
- neighbours: int32 [64, 4, 2, 6, 16], P(('win', 'dx'), 'dy', 'dz'), parts along dimension 0, may hold values from 0 to 161, as said below
- counts: int32 [64, 4, 2, 6], P(('win', 'dx'), 'dy', 'dz'), parts along dimension 0, may hold values from 1 to 16, as said below
- sigma_table: float32 [32], replicated, may hold values from 0.8 to 1.2
- depth_table: float32 [32], replicated, may hold values from 0.002 to 0.03
- charge_table: float32 [32], replicated, may hold values from -1 to 1
- domain_edge: float32 [3], replicated, may hold values from 1 to 1.12
- coupling: float32 [2], P('win'), parts along dimension 0, may hold values from 0.1 to 0.9
Outputs:
- forces: float32 [3, 64, 4, 2, 768], P(None, ('win', 'dx'), 'dy', 'dz'), parts along dimension 1
- energy: float32 [2], P('win'), parts along dimension 0
- dhdl: float32 [2], P('win'), parts along dimension 0
There are 2 independent parts, one for each index of `win`. A program takes and returns all parts, laid end to end along the dimension named above; an argument that names none is the same for every part. Nothing has to cross between parts.
Inputs may be any that keep to these rules, and one draw needn't show every extreme that they name: `leaving`: each domain lists 2 * 16 distinct slots: the first 16 leave toward the next domain, the last 16 toward the previous one. `neighbours`: each list holds 16 distinct ghost block numbers; entries at or past the block's count are valid numbers and are not used. `counts`: some block lists exactly 16 blocks in every draw.
All inputs are finite; a program needn't handle non-finite values.
Results may differ from a plain program's by a relative error of at most 0.0003.
Values sent between devices are 32-bit elements; how exact they have to be, the bound alone decides.
A program may use at most 64 MiB of HBM per device.

v0:
```python
import jax
import jax.numpy as jnp
from jax import lax
from jax.sharding import PartitionSpec as P

soft_base = 0.3
soft_alpha = 0.5
charge_base = 0.3
charge_alpha = 0.5
coulomb = 0.1


def passed_along(array, axis, by):
    devices = lax.axis_size(axis)
    return lax.ppermute(array, axis, [(i, (i + by) % devices) for i in range(devices)])


def extended(block, sides, width):
    for axis, dim in sides:
        count = lax.axis_size(axis)
        forward = [(i, i + 1) for i in range(count - 1)]
        forward.append((count - 1, 0))
        backward = [(target, source) for source, target in forward]
        low = lax.ppermute(
            lax.slice_in_dim(block, block.shape[dim] - width, None, axis=dim), axis, forward
        )
        high = lax.ppermute(lax.slice_in_dim(block, 0, width, axis=dim), axis, backward)
        block = jnp.concatenate([low, block, high], axis=dim)
    return block


def swapped(block, axis, bit):
    count = lax.axis_size(axis)
    route = []
    for low in range(count):
        high = low | 1 << bit
        if high != low and high < count:
            route += [(low, high), (high, low)]
    return lax.ppermute(block, axis, route)


def by_axis(array, axes):
    for axis in axes:
        array = lax.psum(array, axis)
    return array


def lookup(table_row, type_ids):
    onehot = type_ids[None, :] == jnp.arange(table_row.shape[0], dtype=jnp.int32)[:, None]
    return jnp.sum(jnp.where(onehot, table_row[:, None], jnp.float32(0.0)), axis=0)


def pair_block(own_block, other_blocks, live_pairs, coupling_value):
    separation = own_block[0:3][None, :, :, None] - other_blocks[:, 0:3][:, :, None, :]
    radius_sq = jnp.sum(separation * separation, axis=1)
    sigma_pair = 0.5 * (own_block[3][None, :, None] + other_blocks[:, 3][:, None, :])
    depth_pair = jnp.sqrt(own_block[4][None, :, None] * other_blocks[:, 4][:, None, :])
    charges = own_block[5][None, :, None] * other_blocks[:, 5][:, None, :]
    flagged = jnp.maximum(own_block[6][None, :, None], other_blocks[:, 6][:, None, :])
    scaled = coupling_value * flagged
    sigma_two = sigma_pair * sigma_pair
    sigma_six = sigma_two * sigma_two * sigma_two
    soft_six = sigma_six * (soft_base + soft_alpha * scaled) + radius_sq * radius_sq * radius_sq
    soft_two = charge_base + charge_alpha * scaled + radius_sq
    inverse_six = 1.0 / soft_six
    energy_lj = (
        4.0
        * depth_pair
        * (sigma_six * sigma_six * inverse_six * inverse_six - sigma_six * inverse_six)
    )
    grad_six = (
        4.0
        * depth_pair
        * (
            sigma_six * inverse_six * inverse_six
            - 2.0 * sigma_six * sigma_six * inverse_six * inverse_six * inverse_six
        )
    )
    energy_coul = coulomb * charges * lax.rsqrt(soft_two)
    grad_two = -0.5 * energy_coul / soft_two
    weight = 1.0 - scaled
    total_pair = energy_lj + energy_coul
    pair_energy = jnp.sum(weight * total_pair * live_pairs)
    pair_dhdl = jnp.sum(
        flagged
        * (-total_pair + weight * (grad_six * sigma_six * soft_alpha + grad_two * charge_alpha))
        * live_pairs
    )
    force_scale = -weight * (6.0 * radius_sq * radius_sq * grad_six + 2.0 * grad_two) * live_pairs
    forces = jnp.sum(force_scale[:, None] * separation, axis=(0, 3))
    return (forces, pair_energy, pair_dhdl)


def block_terms(ghost_rows, listed_blocks, list_count, block_id, block_total, coupling_value):
    centre = 13 * block_total + block_id
    own_block = lax.dynamic_index_in_dim(ghost_rows, centre, 0, keepdims=False)
    other_blocks = jnp.take(ghost_rows, listed_blocks, axis=0)
    valid_slot = (jnp.arange(listed_blocks.shape[0], dtype=jnp.int32) < list_count).astype(
        jnp.float32
    )
    is_self = (listed_blocks == centre).astype(jnp.float32)[:, None, None] * jnp.eye(
        128, dtype=jnp.float32
    )[None]
    live_pairs = valid_slot[:, None, None] * (1.0 - is_self)
    return pair_block(own_block, other_blocks, live_pairs, coupling_value)


def on_device(
    fraction,
    atom_type,
    perturbed,
    leaving,
    neighbours,
    counts,
    sigma_table,
    depth_table,
    charge_table,
    domain_edge,
    coupling,
):
    atom_count = fraction.shape[-1]
    block_total = atom_count // 128
    spacing = float(atom_count) ** (1.0 / 3.0)
    type_ids = atom_type.reshape(atom_count)
    payload = jnp.concatenate(
        [
            fraction.reshape(3, atom_count),
            lookup(sigma_table, type_ids)[None],
            lookup(depth_table, type_ids)[None],
            lookup(charge_table, type_ids)[None],
            perturbed.reshape(1, atom_count).astype(jnp.float32),
        ],
        axis=0,
    )
    leave_slots = leaving.reshape(2, -1)
    shift_x = jnp.zeros((7, 1), jnp.float32).at[0].set(1.0)
    upward = payload[:, leave_slots[0]]
    downward = payload[:, leave_slots[1]]
    from_below = passed_along(upward, "dx", 1) - shift_x
    from_above = passed_along(downward, "dx", -1) + shift_x
    moved = payload.at[:, leave_slots[1]].set(from_below).at[:, leave_slots[0]].set(from_above)
    domain_block = moved.reshape(7, 1, 1, 1, atom_count)
    ghost_plane = extended(domain_block, (("dx", 1), ("dy", 2)), 1)
    partner = swapped(ghost_plane, "dz", 0)
    ghost_cells = jnp.concatenate([partner, ghost_plane, partner], axis=3)
    image_steps = jnp.arange(3, dtype=jnp.float32) - 1.0
    position = jnp.stack(
        [
            (ghost_cells[0] + image_steps[:, None, None, None]) * domain_edge[0] * spacing,
            (ghost_cells[1] + image_steps[None, :, None, None]) * domain_edge[1] * spacing,
            (ghost_cells[2] + image_steps[None, None, :, None]) * domain_edge[2] * spacing,
        ],
        axis=0,
    )
    ghost_all = jnp.concatenate([position, ghost_cells[3:]], axis=0)
    ghost_rows = (
        ghost_all.reshape(7, 27, block_total, 128)
        .transpose(1, 2, 0, 3)
        .reshape(27 * block_total, 7, 128)
    )
    listed = neighbours.reshape(block_total, -1)
    listed_count = counts.reshape(block_total)
    coupling_value = coupling[0]

    def one_block(block_id):
        return block_terms(
            ghost_rows,
            listed[block_id],
            listed_count[block_id],
            block_id,
            block_total,
            coupling_value,
        )

    forces, energies, dhdls = lax.map(one_block, jnp.arange(block_total, dtype=jnp.int32))
    forces = forces.transpose(1, 0, 2).reshape(3, 1, 1, 1, atom_count)
    window_energy, window_dhdl = (
        by_axis(jnp.sum(energies), ("dx", "dy", "dz")),
        by_axis(jnp.sum(dhdls), ("dx", "dy", "dz")),
    )
    slot_total = jnp.float32(
        atom_count * lax.axis_size("dx") * lax.axis_size("dy") * lax.axis_size("dz")
    )
    energy = (0.5 * window_energy / slot_total).reshape(1)
    dhdl = (0.5 * window_dhdl / slot_total).reshape(1)
    return (forces, energy, dhdl)


def solution(mesh):
    return jax.shard_map(
        on_device,
        mesh=mesh,
        in_specs=(
            P(None, ("win", "dx"), "dy", "dz", None),
            P(("win", "dx"), "dy", "dz", None),
            P(("win", "dx"), "dy", "dz", None),
            P(("win", "dx"), "dy", "dz", None, None),
            P(("win", "dx"), "dy", "dz", None, None),
            P(("win", "dx"), "dy", "dz", None),
            P(),
            P(),
            P(),
            P(),
            P("win"),
        ),
        out_specs=(P(None, ("win", "dx"), "dy", "dz", None), P("win"), P("win")),
        check_vma=False,
    )
```

profile of v0, /device:TPU:33, one launch (start us, length us, event | category | flops | bytes accessed | tf_op | source)
XLA Modules:
  0.0 236.6 jit_solution(10978817934598809103)
XLA Ops:
  0.6 0.8 fusion.44
  2.8 0.8 select_reduce_fusion
  5.1 5.3 %collective-permute-start = (f32[7,16]{0,1:T(8,128)S(1)}, f32[7,16]{0,1:T(8,128)S(1)}, u32[]{:S(2)}, u32[]{:S(2)}) collective-permute-start(f32[7,16]{0,1:T(8,128)S(1)} %bitcast.113), channel_id=1, source_target_pairs={{0,8},{8,16},{16,24},{24,32},{32,40},{40,48},{48,56},{56,64},{64,7... | collective-permute-start | bytes 1352 | tf_op jit(solution)/shard_map/ppermute | solution.py:15
  11.0 42.6 %collective-permute-start.1 = (f32[7,16]{0,1:T(8,128)S(1)}, f32[7,16]{0,1:T(8,128)S(1)}, u32[]{:S(2)}, u32[]{:S(2)}) collective-permute-start(f32[7,16]{0,1:T(8,128)S(1)} %bitcast.112), channel_id=1, source_target_pairs={{0,248},{8,0},{16,8},{24,16},{32,24},{40,32},{48,40},{56,48},{64,5... | collective-permute-start | bytes 1352 | tf_op jit(solution)/shard_map/ppermute | solution.py:15
  53.6 0.9 scatter_custom_fusion
  54.6 0.8 scatter_custom_fusion.1
  55.4 4.6 %collective-permute-start.3 = (f32[7,1,1,1,768]{0,4,3,2,1:T(8,128)S(1)}, f32[7,1,1,1,768]{0,4,3,2,1:T(8,128)S(1)}, u32[]{:S(2)}, u32[]{:S(2)}) collective-permute-start(f32[7,1,1,1,768]{0,4,3,2,1:T(8,128)S(1)} %bitcast.97), channel_id=1, source_target_pairs={{8,0},{16,8},{24,16},{32,24},{40,32},{48,40},{56,48},{64,56},{72,6... | collective-permute-start | bytes 64520 | tf_op jit(solution)/shard_map/ppermute | solution.py:27
  60.0 2.0 collective-permute-start.2
  62.1 4.6 %collective-permute-done.3 = f32[7,1,1,1,768]{0,4,3,2,1:T(8,128)S(1)} collective-permute-done((f32[7,1,1,1,768]{0,4,3,2,1:T(8,128)S(1)}, f32[7,1,1,1,768]{0,4,3,2,1:T(8,128)S(1)}, u32[]{:S(2)}, u32[]{:S(2)}) %collective-permute-start.3) | collective-permute-done | bytes 21536 | tf_op jit(solution)/shard_map/ppermute | solution.py:27
  66.9 4.9 %collective-permute-done.2 = f32[7,1,1,1,768]{0,4,3,2,1:T(8,128)S(1)} collective-permute-done((f32[7,1,1,1,768]{0,4,3,2,1:T(8,128)S(1)}, f32[7,1,1,1,768]{0,4,3,2,1:T(8,128)S(1)}, u32[]{:S(2)}, u32[]{:S(2)}) %collective-permute-start.2) | collective-permute-done | bytes 21536 | tf_op jit(solution)/shard_map/ppermute | solution.py:24
  72.0 4.8 %collective-permute-start.5 = (f32[7,3,1,1,768]{4,3,2,1,0:T(1,128)S(1)}, f32[7,3,1,1,768]{4,3,2,1,0:T(1,128)S(1)}, u32[]{:S(2)}, u32[]{:S(2)}) collective-permute-start(f32[7,3,1,1,768]{4,3,2,1,0:T(1,128)S(1)} %pad_maximum_fusion.2), channel_id=1, source_target_pairs={{2,0},{4,2},{6,4},{0,6},{3,1},{5,3},{7,5},{1,7},{10,8},{12,10},{14... | collective-permute-start | bytes 193544 | tf_op jit(solution)/shard_map/ppermute | solution.py:27
  76.8 2.0 collective-permute-start.4
  78.9 4.2 %collective-permute-done.4 = f32[7,3,1,1,768]{4,3,2,1,0:T(1,128)S(1)} collective-permute-done((f32[7,3,1,1,768]{4,3,2,1,0:T(1,128)S(1)}, f32[7,3,1,1,768]{4,3,2,1,0:T(1,128)S(1)}, u32[]{:S(2)}, u32[]{:S(2)}) %collective-permute-start.4) | collective-permute-done | bytes 64544 | tf_op jit(solution)/shard_map/ppermute | solution.py:24
  83.3 6.3 %collective-permute-start.6 = (f32[7,3,3,1,768]{4,3,2,1,0:T(1,128)S(1)}, f32[7,3,3,1,768]{4,3,2,1,0:T(1,128)S(1)}, u32[]{:S(2)}, u32[]{:S(2)}) collective-permute-start(f32[7,3,3,1,768]{4,3,2,1,0:T(1,128)S(1)} %pad_maximum_fusion.1), channel_id=1, source_target_pairs={{0,1},{1,0},{2,3},{3,2},{4,5},{5,4},{6,7},{7,6},{8,9},{9,8},{10,11... | collective-permute-start | bytes 580616 | tf_op jit(solution)/shard_map/ppermute | solution.py:39
  90.8 2.3 fusion.34
  93.4 72.7 %while.17 = (s32[]{:T(128)}, f32[6,3,128]{2,1,0:T(4,128)S(1)}, f32[6]{0:T(128)S(1)}, f32[6]{0:T(128)S(1)}, f32[]{:T(128)}, /*index=5*/s32[6]{0:T(128)S(1)}, f32[...) while((s32[]{:T(128)}, f32[6,3,128]{2,1,0:T(4,128)S(1)}, ...), condition=%wide.region_10.11_spmd, body=%wide.region_5.10_spmd.sunk | while | flops 20495192 | bytes 4781457 | solution.py:175
  99.7 3.8 %fusion.57 = (f32[]{:T(128)}, f32[]{:T(128)}, f32[16,128,128]{2,1,0:T(8,128)S(1)}) fusion(f32[128,128]{1,0:T(8,128)S(1)} %fusion.53, f32[16]{0:T(128)S(1)} %get-tuple-element.253, f32[16]{0:T(128)S(1)} %get-tuple-element.254, f32[16,128]{1,0:T(8,128)S(1)} %bitcast.104, f32[128]{0:T(128)S(1)} %get-tuple-element.257, f32[16,128]{1,0:T(8,128)S(1)} %bitcast.105, ...), kind=kLoop, calls=%fused_computation.33.clone.1 | loop fusion | flops 15990782 | bytes 2197644 | tf_op jit(solution)/shard_map/while/body/eval_jaxpr/reduce_sum | solution.py:84
  104.0 0.8 dynamic_update_slice.25
  104.8 0.8 dynamic_update_slice.26
  111.8 3.8 %fusion.57 = (f32[]{:T(128)}, f32[]{:T(128)}, f32[16,128,128]{2,1,0:T(8,128)S(1)}) fusion(f32[128,128]{1,0:T(8,128)S(1)} %fusion.53, f32[16]{0:T(128)S(1)} %get-tuple-element.253, f32[16]{0:T(128)S(1)} %get-tuple-element.254, f32[16,128]{1,0:T(8,128)S(1)} %bitcast.104, f32[128]{0:T(128)S(1)} %get-tuple-element.257, f32[16,128]{1,0:T(8,128)S(1)} %bitcast.105, ...), kind=kLoop, calls=%fused_computation.33.clone.1 | loop fusion | flops 15990782 | bytes 2197644 | tf_op jit(solution)/shard_map/while/body/eval_jaxpr/reduce_sum | solution.py:84
  116.2 0.8 dynamic_update_slice.25
  124.0 3.8 %fusion.57 = (f32[]{:T(128)}, f32[]{:T(128)}, f32[16,128,128]{2,1,0:T(8,128)S(1)}) fusion(f32[128,128]{1,0:T(8,128)S(1)} %fusion.53, f32[16]{0:T(128)S(1)} %get-tuple-element.253, f32[16]{0:T(128)S(1)} %get-tuple-element.254, f32[16,128]{1,0:T(8,128)S(1)} %bitcast.104, f32[128]{0:T(128)S(1)} %get-tuple-element.257, f32[16,128]{1,0:T(8,128)S(1)} %bitcast.105, ...), kind=kLoop, calls=%fused_computation.33.clone.1 | loop fusion | flops 15990782 | bytes 2197644 | tf_op jit(solution)/shard_map/while/body/eval_jaxpr/reduce_sum | solution.py:84
  128.3 0.8 dynamic_update_slice.25
  136.1 3.8 %fusion.57 = (f32[]{:T(128)}, f32[]{:T(128)}, f32[16,128,128]{2,1,0:T(8,128)S(1)}) fusion(f32[128,128]{1,0:T(8,128)S(1)} %fusion.53, f32[16]{0:T(128)S(1)} %get-tuple-element.253, f32[16]{0:T(128)S(1)} %get-tuple-element.254, f32[16,128]{1,0:T(8,128)S(1)} %bitcast.104, f32[128]{0:T(128)S(1)} %get-tuple-element.257, f32[16,128]{1,0:T(8,128)S(1)} %bitcast.105, ...), kind=kLoop, calls=%fused_computation.33.clone.1 | loop fusion | flops 15990782 | bytes 2197644 | tf_op jit(solution)/shard_map/while/body/eval_jaxpr/reduce_sum | solution.py:84
  140.4 0.8 dynamic_update_slice.25
  148.2 3.8 %fusion.57 = (f32[]{:T(128)}, f32[]{:T(128)}, f32[16,128,128]{2,1,0:T(8,128)S(1)}) fusion(f32[128,128]{1,0:T(8,128)S(1)} %fusion.53, f32[16]{0:T(128)S(1)} %get-tuple-element.253, f32[16]{0:T(128)S(1)} %get-tuple-element.254, f32[16,128]{1,0:T(8,128)S(1)} %bitcast.104, f32[128]{0:T(128)S(1)} %get-tuple-element.257, f32[16,128]{1,0:T(8,128)S(1)} %bitcast.105, ...), kind=kLoop, calls=%fused_computation.33.clone.1 | loop fusion | flops 15990782 | bytes 2197644 | tf_op jit(solution)/shard_map/while/body/eval_jaxpr/reduce_sum | solution.py:84
  152.5 0.8 dynamic_update_slice.25
  160.3 3.8 %fusion.57 = (f32[]{:T(128)}, f32[]{:T(128)}, f32[16,128,128]{2,1,0:T(8,128)S(1)}) fusion(f32[128,128]{1,0:T(8,128)S(1)} %fusion.53, f32[16]{0:T(128)S(1)} %get-tuple-element.253, f32[16]{0:T(128)S(1)} %get-tuple-element.254, f32[16,128]{1,0:T(8,128)S(1)} %bitcast.104, f32[128]{0:T(128)S(1)} %get-tuple-element.257, f32[16,128]{1,0:T(8,128)S(1)} %bitcast.105, ...), kind=kLoop, calls=%fused_computation.33.clone.1 | loop fusion | flops 15990782 | bytes 2197644 | tf_op jit(solution)/shard_map/while/body/eval_jaxpr/reduce_sum | solution.py:84
  164.6 0.8 dynamic_update_slice.25
  167.9 39.8 %all-reduce = (f32[]{:T(128)}, f32[]{:T(128)}) all-reduce(f32[]{:T(128)} %reduce_sum.96, f32[]{:T(128)} %reduce_sum.97), channel_id=1, replica_groups=mesh['win'=2,'dx'=32,'dy'=4,'dz'=2] {'dx'}, use_global_device_ids=true, to_apply=%region_12.13 | all-reduce | flops 2 | bytes 16 | tf_op jit(solution)/shard_map/psum | solution.py:44
  207.7 6.7 %all-reduce.1 = (f32[]{:T(128)}, f32[]{:T(128)}) all-reduce(f32[]{:T(128)} %get-tuple-element.156, f32[]{:T(128)} %get-tuple-element.157), channel_id=1, replica_groups=mesh['win'=2,'dx'=32,'dy'=4,'dz'=2] {'dy'}, use_global_device_ids=true, to_apply=%region_13.14 | all-reduce | flops 2 | bytes 16 | tf_op jit(solution)/shard_map/psum | solution.py:44
  214.4 18.6 %all-reduce.2 = (f32[]{:T(128)}, f32[]{:T(128)}) all-reduce(f32[]{:T(128)} %get-tuple-element.158, f32[]{:T(128)} %get-tuple-element.159), channel_id=1, replica_groups=mesh['win'=2,'dx'=32,'dy'=4,'dz'=2] {'dz'}, use_global_device_ids=true, to_apply=%region_14.15 | all-reduce | flops 2 | bytes 16 | tf_op jit(solution)/shard_map/psum | solution.py:44
  (145 shorter events, 31.8 us)
Async XLA Ops:
  0.6 53.9 %copy-start.2 = (f32[7]{0:T(128)S(1)}, f32[7]{0:T(128)}, u32[]{:S(2)}) copy-start(f32[7]{0:T(128)} %constant.159.clone.1) | copy-start | bytes 88
  5.1 48.4 %collective-permute-start = (f32[7,16]{0,1:T(8,128)S(1)}, f32[7,16]{0,1:T(8,128)S(1)}, u32[]{:S(2)}, u32[]{:S(2)}) collective-permute-start(f32[7,16]{0,1:T(8,128)S(1)} %bitcast.113), channel_id=1, source_target_pairs={{0,8},{8,16},{16,24},{24,32},{32,40},{40,48},{48,56},{56,64},{64,7... | collective-permute-start | bytes 1352 | tf_op jit(solution)/shard_map/ppermute | solution.py:15
  11.0 67.9 %copy-start.1 = (s32[1,1,1,6,16]{4,2,3,1,0:T(1,128)S(1)}, s32[1,1,1,6,16]{4,2,3,1,0:T(1,128)}, u32[]{:S(2)}) copy-start(s32[1,1,1,6,16]{4,2,3,1,0:T(1,128)} %param.19) | copy-start | bytes 1156
  11.0 43.6 %collective-permute-start.1 = (f32[7,16]{0,1:T(8,128)S(1)}, f32[7,16]{0,1:T(8,128)S(1)}, u32[]{:S(2)}, u32[]{:S(2)}) collective-permute-start(f32[7,16]{0,1:T(8,128)S(1)} %bitcast.112), channel_id=1, source_target_pairs={{0,248},{8,0},{16,8},{24,16},{32,24},{40,32},{48,40},{56,48},{64,5... | collective-permute-start | bytes 1352 | tf_op jit(solution)/shard_map/ppermute | solution.py:15
  54.5 35.0 %copy-start = (f32[3]{0:T(128)S(1)}, f32[3]{0:T(128)}, u32[]{:S(2)}) copy-start(f32[3]{0:T(128)} %param.24) | copy-start | bytes 40
  55.4 11.4 %collective-permute-start.3 = (f32[7,1,1,1,768]{0,4,3,2,1:T(8,128)S(1)}, f32[7,1,1,1,768]{0,4,3,2,1:T(8,128)S(1)}, u32[]{:S(2)}, u32[]{:S(2)}) collective-permute-start(f32[7,1,1,1,768]{0,4,3,2,1:T(8,128)S(1)} %bitcast.97), channel_id=1, source_target_pairs={{8,0},{16,8},{24,16},{32,24},{40,32},{48,40},{56,48},{64,56},{72,6... | collective-permute-start | bytes 64520 | tf_op jit(solution)/shard_map/ppermute | solution.py:27
  60.0 11.8 %collective-permute-start.2 = (f32[7,1,1,1,768]{0,4,3,2,1:T(8,128)S(1)}, f32[7,1,1,1,768]{0,4,3,2,1:T(8,128)S(1)}, u32[]{:S(2)}, u32[]{:S(2)}) collective-permute-start(f32[7,1,1,1,768]{0,4,3,2,1:T(8,128)S(1)} %bitcast.98), channel_id=1, source_target_pairs={{0,8},{8,16},{16,24},{24,32},{32,40},{40,48},{48,56},{56,64},{64,7... | collective-permute-start | bytes 64520 | tf_op jit(solution)/shard_map/ppermute | solution.py:24
  72.0 6.8 %collective-permute-start.5 = (f32[7,3,1,1,768]{4,3,2,1,0:T(1,128)S(1)}, f32[7,3,1,1,768]{4,3,2,1,0:T(1,128)S(1)}, u32[]{:S(2)}, u32[]{:S(2)}) collective-permute-start(f32[7,3,1,1,768]{4,3,2,1,0:T(1,128)S(1)} %pad_maximum_fusion.2), channel_id=1, source_target_pairs={{2,0},{4,2},{6,4},{0,6},{3,1},{5,3},{7,5},{1,7},{10,8},{12,10},{14... | collective-permute-start | bytes 193544 | tf_op jit(solution)/shard_map/ppermute | solution.py:27
  76.8 6.2 %collective-permute-start.4 = (f32[7,3,1,1,768]{4,3,2,1,0:T(1,128)S(1)}, f32[7,3,1,1,768]{4,3,2,1,0:T(1,128)S(1)}, u32[]{:S(2)}, u32[]{:S(2)}) collective-permute-start(f32[7,3,1,1,768]{4,3,2,1,0:T(1,128)S(1)} %pad_maximum_fusion.2), channel_id=1, source_target_pairs={{0,2},{2,4},{4,6},{6,0},{1,3},{3,5},{5,7},{7,1},{8,10},{10,12},{12... | collective-permute-start | bytes 193544 | tf_op jit(solution)/shard_map/ppermute | solution.py:24
  83.3 7.3 %collective-permute-start.6 = (f32[7,3,3,1,768]{4,3,2,1,0:T(1,128)S(1)}, f32[7,3,3,1,768]{4,3,2,1,0:T(1,128)S(1)}, u32[]{:S(2)}, u32[]{:S(2)}) collective-permute-start(f32[7,3,3,1,768]{4,3,2,1,0:T(1,128)S(1)} %pad_maximum_fusion.1), channel_id=1, source_target_pairs={{0,1},{1,0},{2,3},{3,2},{4,5},{5,4},{6,7},{7,6},{8,9},{9,8},{10,11... | collective-permute-start | bytes 580616 | tf_op jit(solution)/shard_map/ppermute | solution.py:39
  90.8 2.7 %copy-start.3 = (s32[1,1,1,6]{3,2,1,0:T(1,128)S(1)}, s32[1,1,1,6]{3,2,1,0:T(1,128)}, u32[]{:S(2)}) copy-start(s32[1,1,1,6]{3,2,1,0:T(1,128)} %param.20) | copy-start | bytes 76
where the time goes:
time: 238 us; the launch traced here: 237 us
  starting transfers between devices  67.4 us (28%)
  blocking collectives  65.1 us (27%)
  other arithmetic  41.6 us (17%)
  local copies, waits for them, and re-layouts  23.9 us (10%)
  loops' own time  20 us (8%)
  waiting for transfers between devices  14.1 us (6%)
  between operations  4.53 us (2%)
    psum x3, blocking collectives, by_axis(): array = lax.psum(array, axis)  65.1 us
    ppermute x2, starting transfers between devices, passed_along(): lax.ppermute(array, axis, [(i, (i + by) % devices) for i in range(devices)])  47.8 us
    reduce_sum x6, other arithmetic, pair_block(): jnp.sum(flagged * (-total_pair + weight * (grad_six * sigma_six * soft_al...  23.1 us
    another operation x1, loops' own time, on_device(): lax.map(one_block, jnp.arange(block_total, dtype=jnp.int32))  20 us
    ppermute x2, starting transfers between devices, extended(): lax.ppermute(lax.slice_in_dim(block, 0, width, axis=dim), axis, backward)  9.45 us
    dynamic_update_slice x18, local copies, waits for them, and re-layouts, on_device(): lax.map(one_block, jnp.arange(block_total, dtype=jnp.int32))  9.16 us
    ppermute x2, waiting for transfers between devices, extended(): lax.ppermute(lax.slice_in_dim(block, block.shape[dim] - width, None, axis...  9.12 us
    ppermute x1, starting transfers between devices, swapped(): return lax.ppermute(block, axis, route)  6.26 us
  transfers between devices with their start and end apart: 7, of which 4 were waited for; matrix products, arithmetic and copies ran while one was open for 1% of the time, Pallas kernels for 0%

commit v1 on v0

v1 whole, which is shorter than its diff:
```python
import math

import jax
import jax.numpy as jnp
from jax import lax
from jax.experimental import pallas as pl
from jax.experimental.pallas import tpu as pltpu
from jax.sharding import PartitionSpec as P

F32 = jnp.float32
BF16 = jnp.bfloat16
MESH = pl.DeviceIdType.MESH
HIGHEST = lax.Precision.HIGHEST

SIGMA_SCALE = 0.5 * 4.0 ** (-1.0 / 6.0)
CHARGE_SCALE = math.sqrt(0.1 / math.sqrt(2.0))
PLANE = [(a, b) for a in (-1, 0, 1) for b in (-1, 0, 1)]
CHUNK = 16


def split3(x):
    high = x.astype(BF16)
    rest = x - high.astype(F32)
    mid = rest.astype(BF16)
    low = (rest - mid.astype(F32)).astype(BF16)
    return high, mid, low


def join3(x):
    return x[0:8] + (x[8:16] + x[16:24])


def pair(own, other):
    dx, dy, dz = own[0] - other[0], own[1] - other[1], own[2] - other[2]
    r2 = dx * dx + dy * dy + dz * dz
    c = jnp.maximum(own[6], other[6])
    h = own[3] + other[3]
    h2 = h * h
    s = h2 * h2 * h2
    r4 = r2 * r2
    inverse = 1.0 / (s * c + r4 * r2)
    u = s * inverse
    root = lax.rsqrt(c + r2)
    t = (own[4] * other[4]) * u
    ty = t * (u - 1.0)
    coul = (own[5] * other[5]) * root
    return (dx, dy, dz), c, r4, inverse, u, root, t, ty, coul


def kernel(
    sizes,
    frac_hbm,
    type_hbm,
    pert_hbm,
    leaving,
    neighbours,
    counts,
    sigma_table,
    depth_table,
    charge_table,
    edge,
    coupling,
    forces_out,
    energy_out,
    dhdl_out,
    pay,
    kinds,
    perts,
    table,
    mig_out,
    mig_in,
    mine,
    theirs,
    ghost,
    own,
    force_acc,
    plane_sums,
    line_sums,
    in_sem,
    mig_send,
    mig_recv,
    halo_send,
    halo_recv,
    over_send,
    over_recv,
    plane_send,
    plane_recv,
    line_send,
    line_recv,
    token,
):
    n_dx, n_dy, n_dz, blocks, listed = sizes
    me_x, me_y, me_z = lax.axis_index("dx"), lax.axis_index("dy"), lax.axis_index("dz")

    def along(a, b, c=0):
        return {
            "dx": lax.rem(me_x + a % n_dx, n_dx),
            "dy": lax.rem(me_y + b % n_dy, n_dy),
            "dz": lax.rem(me_z + c, n_dz),
        }

    def signal(semaphore, device):
        pl.semaphore_signal(semaphore, inc=1, device_id=device, device_id_type=MESH)

    peers = [(b, c) for b in range(n_dy) for c in range(n_dz) if (b, c) != (0, 0)]
    near = [(a, b, 0) for a, b in PLANE if a != 0]
    near += [(0, b, c) for b, c in peers]
    barrier = pltpu.get_barrier_semaphore()
    for device in near:
        signal(barrier, along(*device))

    copies = []
    for q in range(blocks):
        lanes = pl.ds(q * 128, 128)
        for k in range(3):
            copies.append((frac_hbm.at[k, 0, 0, 0, lanes], pay.at[q, k]))
        copies.append((type_hbm.at[0, 0, 0, lanes], kinds.at[q]))
        copies.append((pert_hbm.at[0, 0, 0, lanes], perts.at[q]))
    copies = [
        pltpu.make_async_copy(src, dst, in_sem.at[i]) for i, (src, dst) in enumerate(copies)
    ]
    for copy in copies:
        copy.start()

    lam = coupling[0]
    sub = lax.broadcasted_iota(jnp.int32, (32, 128), 0)
    lane8 = lax.broadcasted_iota(jnp.int32, (8, 128), 1)
    gather_slots = jnp.zeros((8, 128), jnp.int32)
    scatter_slots = jnp.zeros((32, 128), jnp.int32)
    for m in range(32):
        down = leaving[0, 0, 0, 1 - m // 16, m % 16]
        home = leaving[0, 0, 0, m // 16, m % 16]
        gather_slots = jnp.where(lane8 == m, down, gather_slots)
        scatter_slots = jnp.where(sub == m, home, scatter_slots)
    gather_slots = jnp.where(lane8 < 32, gather_slots, -1)

    for copy in copies:
        copy.wait()
    kind = kinds[0:blocks, :]
    sigma = jnp.zeros((blocks, 128), F32)
    depth = jnp.zeros((blocks, 128), F32)
    charge = jnp.zeros((blocks, 128), F32)
    for k in range(sigma_table.shape[0]):
        hit = kind == k
        sigma = jnp.where(hit, sigma_table[k], sigma)
        depth = jnp.where(hit, depth_table[k], depth)
        charge = jnp.where(hit, charge_table[k], charge)
    flag = perts[0:blocks, :].astype(F32)
    table[0] = sigma * SIGMA_SCALE
    table[1] = jnp.sqrt(depth)
    table[2] = charge * CHARGE_SCALE
    table[3] = 0.15 + (0.25 * lam) * flag
    table[4] = flag
    for q in range(blocks):
        for k in range(5):
            pay[q, 3 + k : 4 + k, :] = table[k, q : q + 1, :]

    rows = lax.broadcasted_iota(jnp.int32, (128, 128), 0)
    gathered = jnp.zeros((24, 128), F32)
    for q in range(blocks):
        pick = (gather_slots[0:1] == rows + q * 128).astype(F32).astype(BF16)
        parts = jnp.concatenate(split3(pay[q]), axis=0)
        gathered += jnp.dot(parts, pick, preferred_element_type=F32)
    mig_out[...] = join3(gathered)

    pl.semaphore_wait(barrier, len(near))
    for a in (-1, 1):
        signal(token.at[0], along(a, 0))
    moves = []
    for i, a in enumerate((1, -1)):
        moves.append(
            pltpu.make_async_remote_copy(
                mig_out, mig_in.at[i], mig_send.at[i], mig_recv.at[i], along(a, 0), MESH
            )
        )
    for move in moves:
        move.start()

    spacing = float(blocks * 128) ** (1.0 / 3.0) * math.sqrt(0.5)
    row8 = lax.broadcasted_iota(jnp.int32, (8, 128), 0)
    scale = jnp.ones((8, 128), F32)
    for k in range(3):
        scale = jnp.where(row8 == k, edge[k] * spacing, scale)

    def placed(tile, a, b, c):
        step = jnp.zeros((8, 128), F32)
        for k, value in enumerate((a, b, c)):
            if value:
                step = jnp.where(row8 == k, float(value), step)
        return (tile + step) * scale

    for move in moves:
        move.wait()
    tile = jnp.where(lane8 < 16, mig_in[1], mig_in[0])
    step_x = jnp.where(row8 == 0, jnp.where(lane8 < 16, 1.0, -1.0), 0.0)
    parts = jnp.concatenate((*split3(tile + step_x), jnp.ones((8, 128), BF16)), axis=0)
    lane32 = lax.broadcasted_iota(jnp.int32, (32, 128), 1)
    for q in range(blocks):
        spread = (scatter_slots == lane32 + q * 128).astype(F32).astype(BF16)
        landed = jnp.dot(parts[:, 0:32], spread, preferred_element_type=F32)
        mine[4, q] = jnp.where(landed[24:32] > 0.5, join3(landed), pay[q])

    sends = []
    for i, (a, b) in enumerate(PLANE):
        if (a, b) != (0, 0):
            sends.append(
                pltpu.make_async_remote_copy(
                    mine.at[4], mine.at[i], halo_send.at[i], halo_recv.at[i], along(-a, -b), MESH
                )
            )
    for send in sends:
        send.start()

    def over(i):
        return pltpu.make_async_remote_copy(
            mine.at[i], theirs.at[i], over_send.at[i], over_recv.at[i], along(0, 0, 1), MESH
        )

    overs = {4: over(4)}
    overs[4].start()
    pl.semaphore_wait(token.at[0], 2)
    for a in (-2, 2):
        signal(token.at[1], along(a, 0))

    center = 13 * blocks
    for q in range(blocks):
        ghost[center + q] = placed(mine[4, q], 0, 0, 0)
    ghost[27 * blocks] = jnp.where(row8 == 3, 1.0, jnp.where(row8 == 6, 0.15, 0.0))
    for q in range(blocks):
        columns = ghost[center + q].T
        for k in range(8):
            own[k, q * 128 : q * 128 + 128, :] = jnp.broadcast_to(
                columns[:, k : k + 1], (128, 128)
            )

    pl.semaphore_wait(token.at[1], 2)
    for a in (-4, 4):
        signal(token.at[2], along(a, 0))
    order = [i for i, (a, b) in enumerate(PLANE) if abs(a) + abs(b) == 1]
    order += [i for i, (a, b) in enumerate(PLANE) if abs(a) + abs(b) == 2]
    by_slot = dict(zip([i for i in range(9) if i != 4], sends))
    for i in order:
        by_slot[i].wait_recv()
        overs[i] = over(i)
        overs[i].start()
        a, b = PLANE[i]
        for q in range(blocks):
            ghost[(3 * i + 1) * blocks + q] = placed(mine[i, q], a, b, 0)
    pl.semaphore_wait(token.at[2], 2)
    for a in (-8, 8):
        signal(token.at[3], along(a, 0))
    for i in [4] + order:
        overs[i].wait_recv()
        a, b = PLANE[i]
        for q in range(blocks):
            for c in (-1, 1):
                ghost[(3 * i + 1 + c) * blocks + q] = placed(theirs[i, q], a, b, c)
    for i in range(9):
        if i != 4:
            by_slot[i].wait_send()
        overs[i].wait_send()

    steps = blocks * 128 // CHUNK
    per_block = 128 // CHUNK
    halves = CHUNK // 8

    def block_number(q, e):
        used = e < counts[0, 0, 0, q]
        return jnp.where(used, neighbours[0, 0, 0, q, e], 27 * blocks)

    def own_rows(k):
        return [
            [own[r, pl.ds(k * CHUNK + 8 * half, 8), :] for r in range(8)] for half in range(halves)
        ]

    def other_rows(q, e):
        number = block_number(q, e)
        return [ghost[number, r : r + 1, :] for r in range(8)]

    def energy_step(k, sums):
        q = k // per_block
        atoms = own_rows(k)
        v_sum, pv_sum, pg_sum = sums
        for e in range(listed):
            other = other_rows(q, e)
            for atom in atoms:
                _, _, _, _, u, root, t, ty, coul = pair(atom, other)
                p = jnp.maximum(atom[7], other[7])
                v = (ty - t) + coul
                g = u * ty + 0.25 * (coul * (root * root))
                v_sum, pv_sum, pg_sum = v_sum + v, pv_sum + p * v, pg_sum + p * g
        return v_sum, pv_sum, pg_sum

    zero = jnp.zeros((8, 128), F32)
    v_sum, pv_sum, pg_sum = lax.fori_loop(0, steps, energy_step, (zero, zero, zero))
    v_row = jnp.sum(v_sum, axis=0, keepdims=True)
    pv_row = jnp.sum(pv_sum, axis=0, keepdims=True)
    pg_row = jnp.sum(pg_sum, axis=0, keepdims=True)
    for q in range(blocks):
        itself = jnp.float32(0.0)
        for e in range(listed):
            itself += jnp.where(block_number(q, e) == center + q, 1.0, 0.0)
        tile = ghost[center + q]
        atom = [tile[r : r + 1] for r in range(8)]
        _, _, _, _, u, root, t, ty, coul = pair(atom, atom)
        v = (ty - t) + coul
        g = u * ty + 0.25 * (coul * (root * root))
        v_row -= itself * v
        pv_row -= itself * (atom[7] * v)
        pg_row -= itself * (atom[7] * g)
    energy_row = v_row - lam * pv_row
    dhdl_row = -pv_row - (0.5 * (1.0 - lam)) * pg_row
    lane1 = lax.broadcasted_iota(jnp.int32, (1, 128), 1)
    energy_row += pltpu.roll(energy_row, 64, 1)
    dhdl_row += pltpu.roll(dhdl_row, 64, 1)
    part = jnp.where(lane1 < 64, energy_row, dhdl_row)

    my_peer = me_y * n_dz + me_z
    plane_sums[my_peer] = part
    plane_copies = []
    for i, (b, c) in enumerate(peers):
        plane_copies.append(
            pltpu.make_async_remote_copy(
                plane_sums.at[my_peer],
                plane_sums.at[my_peer],
                plane_send.at[i],
                plane_recv.at[i],
                along(0, b, c),
                MESH,
            )
        )
    for copy in plane_copies:
        copy.start()

    def force_step(k, carry):
        q = k // per_block
        atoms = own_rows(k)
        sums = [[jnp.zeros((8, 128), F32)] * 3 for _ in atoms]
        twelve = [atom[4] * 12.0 for atom in atoms]
        atoms = [atom[:4] + [big] + atom[5:] for atom, big in zip(atoms, twelve)]
        for e in range(listed):
            other = other_rows(q, e)
            for half, atom in enumerate(atoms):
                d, c, r4, inverse, _, root, _, ty, coul = pair(atom, other)
                f = (r4 * inverse) * ty + coul * (root * root)
                f *= 1.6 - 4.0 * c
                sums[half] = [total + f * part for total, part in zip(sums[half], d)]
        for half, totals in enumerate(sums):
            for axis, total in enumerate(totals):
                force_acc[axis, pl.ds(k * CHUNK + 8 * half, 8), :] = total
        return carry

    first = steps // 3
    lax.fori_loop(0, first, force_step, 0)
    for copy in plane_copies:
        copy.wait()
    total = plane_sums[0]
    for i in range(1, n_dy * n_dz):
        total = total + plane_sums[i]
    line_sums[me_x] = total
    pl.semaphore_wait(token.at[3], 2)
    line_copies = []
    for d in range(1, n_dx):
        line_copies.append(
            pltpu.make_async_remote_copy(
                line_sums.at[me_x],
                line_sums.at[me_x],
                line_send.at[d],
                line_recv.at[d],
                along(d, 0),
                MESH,
            )
        )
    for copy in line_copies:
        copy.start()

    lax.fori_loop(first, steps, force_step, 0)
    ones = jnp.ones((8, 128), F32)
    for q in range(blocks):
        for axis in range(3):
            sums = lax.dot_general(
                ones,
                force_acc[axis, q * 128 : q * 128 + 128, :],
                (((1,), (1,)), ((), ())),
                precision=HIGHEST,
                preferred_element_type=F32,
            )
            forces_out[axis, 0, 0, :, q * 128 : q * 128 + 128] = sums[0:1] * math.sqrt(0.5)

    for copy in line_copies:
        copy.wait()
    total = line_sums[0]
    for i in range(1, n_dx):
        total = total + line_sums[i]
    norm = 0.5 / (blocks * 128 * n_dx * n_dy * n_dz)
    energy_out[0] = jnp.sum(jnp.where(lane1 < 64, total, 0.0)) * norm
    dhdl_out[0] = jnp.sum(jnp.where(lane1 < 64, 0.0, total)) * norm


def on_device(
    fraction,
    atom_type,
    perturbed,
    leaving,
    neighbours,
    counts,
    sigma_table,
    depth_table,
    charge_table,
    domain_edge,
    coupling,
):
    n_dx, n_dy, n_dz = (lax.axis_size(axis) for axis in ("dx", "dy", "dz"))
    atoms = fraction.shape[-1]
    blocks = atoms // 128
    sizes = (n_dx, n_dy, n_dz, blocks, neighbours.shape[-1])
    hbm = pl.BlockSpec(memory_space=pl.ANY)
    smem = pl.BlockSpec(memory_space=pltpu.SMEM)
    dma, regular = pltpu.SemaphoreType.DMA, pltpu.SemaphoreType.REGULAR
    return pl.pallas_call(
        lambda *refs: kernel(sizes, *refs),
        out_shape=(
            jax.ShapeDtypeStruct(fraction.shape, F32),
            jax.ShapeDtypeStruct((1,), F32),
            jax.ShapeDtypeStruct((1,), F32),
        ),
        in_specs=[hbm] * 3 + [smem] * 8,
        out_specs=(pl.BlockSpec(memory_space=pltpu.VMEM), smem, smem),
        scratch_shapes=[
            pltpu.VMEM((blocks, 8, 128), F32),
            pltpu.VMEM((8, 128), jnp.int32),
            pltpu.VMEM((8, 128), jnp.int32),
            pltpu.VMEM((5, blocks, 128), F32),
            pltpu.VMEM((8, 128), F32),
            pltpu.VMEM((2, 8, 128), F32),
            pltpu.VMEM((9, blocks, 8, 128), F32),
            pltpu.VMEM((9, blocks, 8, 128), F32),
            pltpu.VMEM((27 * blocks + 1, 8, 128), F32),
            pltpu.VMEM((8, atoms, 128), F32),
            pltpu.VMEM((3, atoms, 128), F32),
            pltpu.VMEM((n_dy * n_dz, 1, 128), F32),
            pltpu.VMEM((n_dx, 1, 128), F32),
            dma((5 * blocks,)),
            dma((2,)),
            dma((2,)),
            dma((9,)),
            dma((9,)),
            dma((9,)),
            dma((9,)),
            dma((n_dy * n_dz,)),
            dma((n_dy * n_dz,)),
            dma((n_dx,)),
            dma((n_dx,)),
            regular((4,)),
        ],
        compiler_params=pltpu.CompilerParams(
            collective_id=0, has_side_effects=True, vmem_limit_bytes=48 * 1024 * 1024
        ),
        name="step",
    )(
        fraction,
        atom_type,
        perturbed,
        leaving,
        neighbours,
        counts,
        sigma_table,
        depth_table,
        charge_table,
        domain_edge,
        coupling,
    )


def solution(mesh):
    return jax.shard_map(
        on_device,
        mesh=mesh,
        in_specs=(
            P(None, ("win", "dx"), "dy", "dz", None),
            P(("win", "dx"), "dy", "dz", None),
            P(("win", "dx"), "dy", "dz", None),
            P(("win", "dx"), "dy", "dz", None, None),
            P(("win", "dx"), "dy", "dz", None, None),
            P(("win", "dx"), "dy", "dz", None),
            P(),
            P(),
            P(),
            P(),
            P("win"),
        ),
        out_specs=(P(None, ("win", "dx"), "dy", "dz", None), P("win"), P("win")),
        check_vma=False,
    )
```

time: 238 us -> 89.5 us (0.38)
  Pallas kernels: 0 us -> 80.9 us
  starting transfers between devices: 67.4 us -> 0 us
  blocking collectives: 65.1 us -> 0 us
  other arithmetic: 41.6 us -> 0 us
  local copies, waits for them, and re-layouts: 23.9 us -> 3.33 us
  loops' own time: 20 us -> 0 us
  waiting for transfers between devices: 14.1 us -> 0 us
    pallas_call x0 -> x1, Pallas kernels: none -> 80.9 us  [on_device(): pl.pallas_call(lambda *refs: kernel(sizes, *refs), out_shape=(jax.ShapeDt...]
    ppermute x7 -> x0, starting transfers between devices: 67.4 us -> none  [the longest x2 47.8 us: passed_along(): lax.ppermute(array, axis, [(i, (i + by) % devices) for i in range(devices)])]
    psum x3 -> x0, blocking collectives: 65.1 us -> none  [by_axis(): array = lax.psum(array, axis)]
    reduce_sum x21 -> x0, other arithmetic: 30.2 us -> none  [the longest x6 23.1 us: pair_block(): jnp.sum(flagged * (-total_pair + weight * (grad_six * sigma_six * soft_al...]
    another operation x1 -> x0, loops' own time: 20 us -> none  [on_device(): lax.map(one_block, jnp.arange(block_total, dtype=jnp.int32))]
    ppermute x7 -> x0, waiting for transfers between devices: 14.1 us -> none  [the longest x2 9.12 us: extended(): lax.ppermute(lax.slice_in_dim(block, block.shape[dim] - width, None, axis...]
    dynamic_update_slice x18 -> x0, local copies, waits for them, and re-layouts: 9.16 us -> none  [on_device(): lax.map(one_block, jnp.arange(block_total, dtype=jnp.int32))]
    dynamic_slice x18 -> x0, local copies, waits for them, and re-layouts: 7.08 us -> none  [the longest x6 3.52 us: one_block(): listed_count[block_id]]
  transfers between devices with their start and end apart: 7 -> 0, of which waited for: 4 -> 0; matrix products, arithmetic and copies ran while one was open for 1% -> 0% of each run, Pallas kernels for 0% -> 0%
where the time goes in v1:
time: 89.5 us; the launch traced here: 89.2 us
  Pallas kernels  80.9 us (90%)
  between operations  4.91 us (5%)
  local copies, waits for them, and re-layouts  3.33 us (4%)
    pallas_call x1, Pallas kernels, on_device(): pl.pallas_call(lambda *refs: kernel(sizes, *refs), out_shape=(jax.ShapeDt...  80.9 us
    unnamed x20, local copies, waits for them, and re-layouts  3.33 us

profile of v1, /device:TPU:33, one launch (start us, length us, event | category | flops | bytes accessed | tf_op | source)
XLA Modules:
  0.0 89.2 jit_solution(6748808685304795224)
XLA Ops:
  0.6 0.0 copy-start.4
  0.6 0.0 copy-start.5
  0.7 0.0 copy-start.6
  1.3 0.0 copy-start.1
  1.3 0.0 copy-start.2
  1.4 0.0 copy-start.3
  1.4 0.7 copy.14.refs_4_
  2.1 0.0 copy-done.4
  2.1 0.0 copy-done.5
  2.1 0.0 copy-done.6
  2.1 0.0 copy-done.1
  2.1 0.0 copy-done.2
  2.1 0.0 copy-done.3
  2.1 0.0 copy-start
  2.1 0.7 copy-done
  2.8 0.0 copy-start.7
  2.8 0.7 copy-done.7
  3.5 0.0 copy-start.8
  3.5 0.7 copy-done.8
  4.1 80.9 %step.1 = (f32[3,1,1,1,768]{4,3,2,1,0:T(1,128)S(1)}, f32[1]{0:T(128)}, f32[1]{0:T(128)}) custom-call(f32[3,1,1,1,768]{4,3,2,1,0:T(1,128)S(1)} %copy-done, s32[1,1,1,768]{3,2,1,0:T(1,128)S(1)} %copy-done.1, s32[1,1,1,768]{3,2,1,0:T(1,128)S(1)} %copy-done.2, s32[1,1,1,2,16]{4,3,2,1,0:T(2,128)S(1)} %copy-done.3, s32[1,1,1,6,16]{4,3,2,1,0:T(8,128)S(1)} %copy.14.refs_4_, ...), custom_call_target="tpu_custom_call" | custom-call | tf_op jit(solution)/shard_map/step/pallas_call | solution.py:420
  85.1 0.6 copy.19
Async XLA Ops:
  0.6 1.4 %copy-start.4 = (s32[1,1,1,6]{3,2,1,0:T(1,128)S(1)}, s32[1,1,1,6]{3,2,1,0:T(1,128)}, u32[]{:S(2)}) copy-start(s32[1,1,1,6]{3,2,1,0:T(1,128)} %refs_5_.1) | copy-start | bytes 76
  0.6 1.4 %copy-start.5 = (f32[32]{0:T(128)S(1)}, f32[32]{0:T(128)}, u32[]{:S(2)}) copy-start(f32[32]{0:T(128)} %refs_6_.1) | copy-start | bytes 388
  0.7 1.4 %copy-start.6 = (f32[32]{0:T(128)S(1)}, f32[32]{0:T(128)}, u32[]{:S(2)}) copy-start(f32[32]{0:T(128)} %refs_7_.1) | copy-start | bytes 388
  1.3 0.7 copy-start.1
  1.3 0.7 copy-start.2
  1.4 0.7 copy-start.3
  2.1 0.7 copy-start
  2.8 0.7 copy-start.7
  3.5 0.7 copy-start.8

commit v2 on v1

v2 whole, which is shorter than its diff:
```python
import math

import jax
import jax.numpy as jnp
from jax import lax
from jax.experimental import pallas as pl
from jax.experimental.pallas import tpu as pltpu
from jax.sharding import PartitionSpec as P

F32 = jnp.float32
BF16 = jnp.bfloat16
MESH = pl.DeviceIdType.MESH

SIGMA_SCALE = 0.5 * 4.0 ** (-1.0 / 6.0)
CHARGE_SCALE = math.sqrt(0.1 / math.sqrt(2.0))
FORCE_SCALE = 12.0 * math.sqrt(0.5)
CENTRE = 4
LEAVE_CENTRE = 7
CHUNK = 16


def split3(x):
    high = x.astype(BF16)
    rest = x - high.astype(F32)
    mid = rest.astype(BF16)
    low = (rest - mid.astype(F32)).astype(BF16)
    return high, mid, low


def join3(x):
    return x[0:8] + (x[8:16] + x[16:24])


def pair(own, other):
    dx, dy, dz = own[0] - other[0], own[1] - other[1], own[2] - other[2]
    r2 = dx * dx + dy * dy + dz * dz
    c = jnp.maximum(own[6], other[6])
    h = own[3] + other[3]
    h2 = h * h
    s = h2 * h2 * h2
    r4 = r2 * r2
    inverse = 1.0 / (s * c + r4 * r2)
    u = s * inverse
    root = lax.rsqrt(c + r2)
    t = (own[4] * other[4]) * u
    ty = t * (u - 1.0)
    coul = (own[5] * other[5]) * root
    return (dx, dy, dz), c, r4, inverse, u, root, t, ty, coul


def kernel(
    sizes,
    frac_hbm,
    type_hbm,
    pert_hbm,
    leaving_hbm,
    neighbours_hbm,
    counts_hbm,
    sigma_hbm,
    depth_hbm,
    charge_hbm,
    edge_hbm,
    coupling_hbm,
    forces_out,
    energy_out,
    dhdl_out,
    leaving,
    neighbours,
    counts,
    sigma_table,
    depth_table,
    charge_table,
    edge,
    coupling,
    kinds,
    perts,
    table,
    raw,
    leavers,
    theirs,
    ghost,
    own,
    force_acc,
    plane_sums,
    line_sums,
    in_sem,
    leave_send,
    leave_recv,
    halo_send,
    halo_recv,
    over_send,
    over_recv,
    plane_send,
    plane_recv,
    line_send,
    line_recv,
    token,
):
    n_dx, n_dy, n_dz, blocks, listed = sizes
    me_x, me_y, me_z = lax.axis_index("dx"), lax.axis_index("dy"), lax.axis_index("dz")

    def along(a, b, c=0):
        return {
            "dx": lax.rem(me_x + a % n_dx, n_dx),
            "dy": lax.rem(me_y + b % n_dy, n_dy),
            "dz": lax.rem(me_z + c, n_dz),
        }

    def signal(semaphore, device):
        pl.semaphore_signal(semaphore, inc=1, device_id=device, device_id_type=MESH)

    copies = [
        (leaving_hbm, leaving),
        (sigma_hbm, sigma_table),
        (depth_hbm, depth_table),
        (charge_hbm, charge_table),
        (coupling_hbm, coupling),
        (edge_hbm, edge),
        (neighbours_hbm, neighbours),
        (counts_hbm, counts),
    ]
    for q in range(blocks):
        lanes = pl.ds(q * 128, 128)
        for k in range(3):
            copies.append((frac_hbm.at[k, 0, 0, 0, lanes], raw.at[CENTRE, q, k]))
        copies.append((type_hbm.at[0, 0, 0, lanes], kinds.at[q]))
        copies.append((pert_hbm.at[0, 0, 0, lanes], perts.at[q]))
    copies = [
        pltpu.make_async_copy(src, dst, in_sem.at[i]) for i, (src, dst) in enumerate(copies)
    ]
    for copy in copies:
        copy.start()

    peers = [(b, c) for b in range(n_dy) for c in range(n_dz) if (b, c) != (0, 0)]
    near = [(a, b, 0) for a in (1, -1, 2, -2) for b in (0, 1, -1)]
    near += [(0, b, c) for b, c in peers]
    barrier = pltpu.get_barrier_semaphore()
    for device in near:
        signal(barrier, along(*device))

    row8 = lax.broadcasted_iota(jnp.int32, (8, 128), 0)
    lane8 = lax.broadcasted_iota(jnp.int32, (8, 128), 1)
    for copy in copies:
        copy.wait()
    lam = coupling[0]
    leave_slots = jnp.full((8, 128), -1, jnp.int32)
    land_slots = jnp.full((8, 128), -1, jnp.int32)
    for m in range(16):
        up, down = leaving[0, 0, 0, 0, m], leaving[0, 0, 0, 1, m]
        leave_slots = jnp.where(lane8 == m, down, jnp.where(lane8 == m + 16, up, leave_slots))
        land_slots = jnp.where(lane8 == m, up, jnp.where(lane8 == m + 16, down, land_slots))
    kind = kinds[0:blocks, :]
    sigma = jnp.zeros((blocks, 128), F32)
    depth = jnp.zeros((blocks, 128), F32)
    charge = jnp.zeros((blocks, 128), F32)
    for k in range(sigma_table.shape[0]):
        hit = kind == k
        sigma = jnp.where(hit, sigma_table[k], sigma)
        depth = jnp.where(hit, depth_table[k], depth)
        charge = jnp.where(hit, charge_table[k], charge)
    flag = perts[0:blocks, :].astype(F32)
    table[0] = sigma * SIGMA_SCALE
    table[1] = jnp.sqrt(depth)
    table[2] = charge * CHARGE_SCALE
    table[3] = flag
    for q in range(blocks):
        for k in range(5):
            raw[CENTRE, q, 3 + k : 4 + k, :] = table[min(k, 3), q : q + 1, :]

    rows = lax.broadcasted_iota(jnp.int32, (128, 128), 0)
    gathered = jnp.zeros((24, 128), F32)
    for q in range(blocks):
        pick = (leave_slots[0:1] == rows + q * 128).astype(F32).astype(BF16)
        parts = jnp.concatenate(split3(raw[CENTRE, q]), axis=0)
        gathered += jnp.dot(parts, pick, preferred_element_type=F32)
    leavers[LEAVE_CENTRE] = jnp.where(row8 == 7, land_slots.astype(F32), join3(gathered))

    pl.semaphore_wait(barrier, len(near))
    leaves, halos = {}, {}
    for a in (1, -1, 2, -2, 0):
        for b in (0, 1, -1):
            if (a, b) != (0, 0):
                i = 3 * (a + 2) + b + 1
                leaves[a, b] = pltpu.make_async_remote_copy(
                    leavers.at[LEAVE_CENTRE],
                    leavers.at[i],
                    leave_send.at[i],
                    leave_recv.at[i],
                    along(-a, -b),
                    MESH,
                )
                leaves[a, b].start()
    for a, b in ((-1, 0), (1, 0), (0, 1), (0, -1), (1, 1), (-1, 1), (1, -1), (-1, -1)):
        i = 3 * (a + 1) + b + 1
        halos[a, b] = pltpu.make_async_remote_copy(
            raw.at[CENTRE],
            raw.at[i],
            halo_send.at[i],
            halo_recv.at[i],
            along(-a, -b),
            MESH,
        )
        halos[a, b].start()
    for a in (-2, 2):
        signal(token.at[0], along(a, 0))

    spacing = float(blocks * 128) ** (1.0 / 3.0) * math.sqrt(0.5)
    scale = jnp.ones((8, 128), F32)
    for k in range(3):
        scale = jnp.where(row8 == k, edge[k] * spacing, scale)
    scale = jnp.where(row8 == 6, 0.25 * lam, jnp.where(row8 == 7, -lam, scale))
    base = jnp.where(row8 == 6, 0.15, jnp.where(row8 == 7, 1.0, 0.0))
    step_z = jnp.where(row8 == 2, scale, 0.0)
    lane32 = lax.broadcasted_iota(jnp.int32, (32, 128), 1).astype(F32)
    step_x = jnp.where(row8 == 0, jnp.where(lane8 < 16, 1.0, -1.0), 0.0)
    ones8 = jnp.ones((8, 128), BF16)
    seen = set()

    def arrived(a, b):
        if (a, b) != (0, 0) and (a, b) not in seen:
            seen.add((a, b))
            leaves[a, b].wait_recv()
        return leavers.at[3 * (a + 2) + b + 1]

    overs = []

    def settle(a, b):
        i = 3 * (a + 1) + b + 1
        here, above, below = arrived(a, b), arrived(a + 1, b), arrived(a - 1, b)
        if (a, b) != (0, 0):
            halos[a, b].wait_recv()
        slots = jnp.broadcast_to(here[...].T[0:32, 7:8], (32, 128))
        tile = jnp.where(lane8 < 16, above[...], below[...]) + step_x
        tile = jnp.where(row8 == 7, pltpu.roll(tile, 1, 0), tile)
        parts = jnp.concatenate((*split3(tile), ones8), axis=0)
        offset = base
        for k, value in enumerate((a, b)):
            if value:
                offset = jnp.where(row8 == k, scale * float(value), offset)
        for q in range(blocks):
            spread = (slots == lane32 + float(q * 128)).astype(F32).astype(BF16)
            landed = jnp.dot(parts[:, 0:32], spread, preferred_element_type=F32)
            moved = jnp.where(landed[24:32] > 0.5, join3(landed), raw[i, q])
            ghost[(3 * i + 1) * blocks + q] = moved * scale + offset
        over = pltpu.make_async_remote_copy(
            ghost.at[pl.ds((3 * i + 1) * blocks, blocks)],
            theirs.at[i],
            over_send.at[i],
            over_recv.at[i],
            along(0, 0, 1),
            MESH,
        )
        over.start()
        overs.append((i, over))

    ghost[27 * blocks] = jnp.where(
        row8 == 3, 1.0, jnp.where(row8 == 6, 0.15, jnp.where(row8 == 7, 1.0, 0.0))
    )
    settle(0, 0)
    center = 13 * blocks
    for q in range(blocks):
        columns = ghost[center + q].T
        for k in range(8):
            own[k, q * 128 : q * 128 + 128, :] = jnp.broadcast_to(
                columns[:, k : k + 1], (128, 128)
            )

    def block_number(q, e):
        used = e < counts[0, 0, 0, q]
        return jnp.where(used, neighbours[0, 0, q, 0, e], 27 * blocks)

    self_sums = [jnp.zeros((1, 128), F32)] * 3
    for q in range(blocks):
        itself = jnp.float32(0.0)
        for e in range(listed):
            itself += jnp.where(block_number(q, e) == center + q, 1.0, 0.0)
        tile = ghost[center + q]
        atom = [tile[r : r + 1] for r in range(8)]
        _, _, _, _, u, root, t, ty, coul = pair(atom, atom)
        v = (ty - t) + coul
        g = u * ty + 0.25 * (coul * (root * root))
        off = 1.0 - atom[7]
        self_sums = [
            total + itself * term for total, term in zip(self_sums, (v, off * v, off * g))
        ]

    for b in (0, 1, -1):
        settle(-1, b)
    pl.semaphore_wait(token.at[0], 2)
    for a in (-4, 4):
        signal(token.at[1], along(a, 0))
    for a, b in ((0, 1), (0, -1), (1, 0), (1, 1), (1, -1)):
        settle(a, b)
    for i, over in overs:
        over.wait_recv()
        for q in range(blocks):
            for c in (-1, 1):
                ghost[(3 * i + 1 + c) * blocks + q] = theirs[i, q] + (step_z * float(c))
    for copy in (*leaves.values(), *halos.values()):
        copy.wait_send()
    for _, over in overs:
        over.wait_send()

    steps = blocks * 128 // CHUNK
    per_block = 128 // CHUNK
    halves = CHUNK // 8

    def pair_step(k, sums):
        q = k // per_block
        atoms = [
            [own[r, pl.ds(k * CHUNK + 8 * half, 8), :] for r in range(8)] for half in range(halves)
        ]
        v_sum, ov_sum, og_sum = sums
        force = [[jnp.zeros((8, 128), F32)] * 3 for _ in atoms]
        for e in range(listed):
            number = block_number(q, e)
            other = [ghost[number, r : r + 1, :] for r in range(8)]
            for half, atom in enumerate(atoms):
                d, _, r4, inverse, u, root, t, ty, coul = pair(atom, other)
                w = jnp.minimum(atom[7], other[7])
                off = 1.0 - w
                v = (ty - t) + coul
                m = coul * (root * root)
                g = u * ty + 0.25 * m
                v_sum, ov_sum, og_sum = v_sum + v, ov_sum + off * v, og_sum + off * g
                f = ((r4 * inverse) * ty + m * (1.0 / 12.0)) * w
                force[half] = [total + f * part for total, part in zip(force[half], d)]
        for half, totals in enumerate(force):
            for axis, total in enumerate(totals):
                force_acc[axis, pl.ds(k * CHUNK + 8 * half, 8), :] = total
        return v_sum, ov_sum, og_sum

    zero = jnp.zeros((8, 128), F32)
    third = steps // 3
    sums = lax.fori_loop(0, third, pair_step, (zero, zero, zero))
    pl.semaphore_wait(token.at[1], 2)
    for a in (-8, 8):
        signal(token.at[2], along(a, 0))
    sums = lax.fori_loop(third, steps, pair_step, sums)
    v_row, ov_row, og_row = (
        jnp.sum(total, axis=0, keepdims=True) - itself for total, itself in zip(sums, self_sums)
    )
    lane1 = lax.broadcasted_iota(jnp.int32, (1, 128), 1)
    energy_row = v_row - ov_row
    dhdl_row = ov_row + (0.5 * (1.0 - lam)) * og_row
    energy_row += pltpu.roll(energy_row, 64, 1)
    dhdl_row += pltpu.roll(dhdl_row, 64, 1)
    part = jnp.where(lane1 < 64, energy_row, dhdl_row)

    my_peer = me_y * n_dz + me_z
    plane_sums[my_peer] = part
    plane_copies = []
    for i, (b, c) in enumerate(peers):
        plane_copies.append(
            pltpu.make_async_remote_copy(
                plane_sums.at[my_peer],
                plane_sums.at[my_peer],
                plane_send.at[i],
                plane_recv.at[i],
                along(0, b, c),
                MESH,
            )
        )
    for copy in plane_copies:
        copy.start()

    ones = jnp.ones((8, 384), BF16)

    def row_sums(axis):
        for q in range(blocks):
            parts = jnp.concatenate(
                split3(force_acc[axis, q * 128 : q * 128 + 128, :]), axis=1
            )
            total = lax.dot_general(
                ones, parts, (((1,), (1,)), ((), ())), preferred_element_type=F32
            )
            forces_out[axis, 0, 0, :, q * 128 : q * 128 + 128] = total[0:1] * FORCE_SCALE

    row_sums(0)
    row_sums(1)
    for copy in plane_copies:
        copy.wait()
    total = plane_sums[0]
    for i in range(1, n_dy * n_dz):
        total = total + plane_sums[i]
    line_sums[me_x] = total
    pl.semaphore_wait(token.at[2], 2)
    line_copies = []
    for d in sorted(range(1, n_dx), key=lambda d: min(d, n_dx - d)):
        line_copies.append(
            pltpu.make_async_remote_copy(
                line_sums.at[me_x],
                line_sums.at[me_x],
                line_send.at[d],
                line_recv.at[d],
                along(d, 0),
                MESH,
            )
        )
    for copy in line_copies:
        copy.start()
    row_sums(2)
    for copy in line_copies:
        copy.wait()
    total = line_sums[0]
    for i in range(1, n_dx):
        total = total + line_sums[i]
    norm = 0.5 / (blocks * 128 * n_dx * n_dy * n_dz)
    energy_out[0] = jnp.sum(jnp.where(lane1 < 64, total, 0.0)) * norm
    dhdl_out[0] = jnp.sum(jnp.where(lane1 < 64, 0.0, total)) * (-norm / lam)


def on_device(
    fraction,
    atom_type,
    perturbed,
    leaving,
    neighbours,
    counts,
    sigma_table,
    depth_table,
    charge_table,
    domain_edge,
    coupling,
):
    n_dx, n_dy, n_dz = (lax.axis_size(axis) for axis in ("dx", "dy", "dz"))
    atoms = fraction.shape[-1]
    blocks = atoms // 128
    sizes = (n_dx, n_dy, n_dz, blocks, neighbours.shape[-1])
    neighbours = neighbours.transpose(0, 1, 3, 2, 4)
    hbm = pl.BlockSpec(memory_space=pltpu.HBM)
    smem = pl.BlockSpec(memory_space=pltpu.SMEM)
    dma, regular = pltpu.SemaphoreType.DMA, pltpu.SemaphoreType.REGULAR
    scalars = (
        leaving,
        neighbours,
        counts,
        sigma_table,
        depth_table,
        charge_table,
        domain_edge,
        coupling,
    )
    return pl.pallas_call(
        lambda *refs: kernel(sizes, *refs),
        out_shape=(
            jax.ShapeDtypeStruct(fraction.shape, F32),
            jax.ShapeDtypeStruct((1,), F32),
            jax.ShapeDtypeStruct((1,), F32),
        ),
        in_specs=[hbm] * 11,
        out_specs=(pl.BlockSpec(memory_space=pltpu.VMEM), smem, smem),
        scratch_shapes=[
            *[pltpu.SMEM(array.shape, array.dtype) for array in scalars],
            pltpu.VMEM((8, 128), jnp.int32),
            pltpu.VMEM((8, 128), jnp.int32),
            pltpu.VMEM((4, blocks, 128), F32),
            pltpu.VMEM((9, blocks, 8, 128), F32),
            pltpu.VMEM((15, 8, 128), F32),
            pltpu.VMEM((9, blocks, 8, 128), F32),
            pltpu.VMEM((27 * blocks + 1, 8, 128), F32),
            pltpu.VMEM((8, atoms, 128), F32),
            pltpu.VMEM((3, atoms, 128), F32),
            pltpu.VMEM((n_dy * n_dz, 1, 128), F32),
            pltpu.VMEM((n_dx, 1, 128), F32),
            dma((8 + 5 * blocks,)),
            dma((15,)),
            dma((15,)),
            dma((9,)),
            dma((9,)),
            dma((9,)),
            dma((9,)),
            dma((n_dy * n_dz,)),
            dma((n_dy * n_dz,)),
            dma((n_dx,)),
            dma((n_dx,)),
            regular((3,)),
        ],
        compiler_params=pltpu.CompilerParams(
            collective_id=0, has_side_effects=True, vmem_limit_bytes=62 * 1024 * 1024
        ),
        name="step",
    )(
        fraction,
        atom_type,
        perturbed,
        leaving,
        neighbours,
        counts,
        sigma_table,
        depth_table,
        charge_table,
        domain_edge,
        coupling,
    )


def solution(mesh):
    return jax.shard_map(
        on_device,
        mesh=mesh,
        in_specs=(
            P(None, ("win", "dx"), "dy", "dz", None),
            P(("win", "dx"), "dy", "dz", None),
            P(("win", "dx"), "dy", "dz", None),
            P(("win", "dx"), "dy", "dz", None, None),
            P(("win", "dx"), "dy", "dz", None, None),
            P(("win", "dx"), "dy", "dz", None),
            P(),
            P(),
            P(),
            P(),
            P("win"),
        ),
        out_specs=(P(None, ("win", "dx"), "dy", "dz", None), P("win"), P("win")),
        check_vma=False,
    )
```

time: 89.5 us -> 83.2 us (0.930)
  Pallas kernels: 80.9 us -> 76.7 us
  local copies, waits for them, and re-layouts: 3.33 us -> 1.3 us
    pallas_call x1, Pallas kernels: 80.9 us -> 76.7 us  [on_device(): pl.pallas_call(lambda *refs: kernel(sizes, *refs), out_shape=(jax.ShapeDt...]
    unnamed x20 -> x1, local copies, waits for them, and re-layouts: 3.33 us -> 1.3 us
where the time goes in v2:
time: 83.2 us; the launch traced here: 82.8 us
  Pallas kernels  76.7 us (92%)
  between operations  4.81 us (6%)
  local copies, waits for them, and re-layouts  1.3 us (2%)
    pallas_call x1, Pallas kernels, on_device(): pl.pallas_call(lambda *refs: kernel(sizes, *refs), out_shape=(jax.ShapeDt...  76.7 us

profile of v2, /device:TPU:33, one launch (start us, length us, event | category | flops | bytes accessed | tf_op | source)
XLA Modules:
  0.0 82.8 jit_solution(13156714188142372622)
XLA Ops:
  1.3 76.7 %step.1 = (f32[3,1,1,1,768]{4,3,2,1,0:T(1,128)}, f32[1]{0:T(128)}, f32[1]{0:T(128)}) custom-call(f32[3,1,1,1,768]{4,3,2,1,0:T(1,128)} %refs_0_.1, s32[1,1,1,768]{3,2,1,0:T(1,128)} %refs_1_.1, s32[1,1,1,768]{3,2,1,0:T(1,128)} %refs_2_.1, s32[1,1,1,2,16]{4,3,2,1,0:T(2,128)} %refs_3_.1, s32[1,1,6,1,16]{4,3,2,1,0:T(1,128)} %bitcast.1, s32[1,1,1,6]{3,2,1,0:T(1,128)} %refs_5_.1, ...), custom_call_target="tpu_custom_call" | custom-call | tf_op jit(solution)/shard_map/step/pallas_call | solution.py:444
  78.0 1.3 %copy.18 = f32[3,1,1,1,768]{4,3,2,1,0:T(1,128)} copy(f32[3,1,1,1,768]{4,3,2,1,0:T(1,128)} %get-tuple-element.6) | data formatting | bytes 18432

commit v3 on v2

--- a/solution.py
+++ b/solution.py
@@ -17,6 +17,7 @@
 CENTRE = 4
 LEAVE_CENTRE = 7
 CHUNK = 16
+LATE_A, LATE_B = 14, 20
 
 
 def split3(x):
@@ -62,6 +63,8 @@
     edge_hbm,
     coupling_hbm,
     forces_out,
+    energy_hbm,
+    dhdl_hbm,
     energy_out,
     dhdl_out,
     leaving,
@@ -73,10 +76,11 @@
     edge,
     coupling,
     kinds,
-    perts,
+    rows_in,
     table,
     raw,
     leavers,
+    landed,
     theirs,
     ghost,
     own,
@@ -84,16 +88,16 @@
     plane_sums,
     line_sums,
     in_sem,
-    leave_send,
+    rows_sem,
+    ici_send,
     leave_recv,
-    halo_send,
     halo_recv,
-    over_send,
     over_recv,
     plane_send,
     plane_recv,
     line_send,
     line_recv,
+    out_sem,
     token,
 ):
     n_dx, n_dy, n_dz, blocks, listed = sizes
@@ -119,17 +123,21 @@
         (neighbours_hbm, neighbours),
         (counts_hbm, counts),
     ]
-    for q in range(blocks):
-        lanes = pl.ds(q * 128, 128)
-        for k in range(3):
-            copies.append((frac_hbm.at[k, 0, 0, 0, lanes], raw.at[CENTRE, q, k]))
-        copies.append((type_hbm.at[0, 0, 0, lanes], kinds.at[q]))
-        copies.append((pert_hbm.at[0, 0, 0, lanes], perts.at[q]))
     copies = [
         pltpu.make_async_copy(src, dst, in_sem.at[i]) for i, (src, dst) in enumerate(copies)
     ]
     for copy in copies:
         copy.start()
+    for q in range(blocks):
+        lanes = pl.ds(q * 128, 128)
+        row_copies = [(frac_hbm.at[k, 0, 0, 0, lanes], raw.at[CENTRE, q, k]) for k in range(3)]
+        row_copies.append((type_hbm.at[0, 0, 0, lanes], kinds.at[q]))
+        row_copies.append((pert_hbm.at[0, 0, 0, lanes], kinds.at[blocks + q]))
+        for src, dst in row_copies:
+            pltpu.make_async_copy(src, dst, rows_sem).start()
+
+    def wait_bytes(ref, semaphore):
+        pltpu.make_async_copy(ref, ref, semaphore).wait()
 
     peers = [(b, c) for b in range(n_dy) for c in range(n_dz) if (b, c) != (0, 0)]
     near = [(a, b, 0) for a in (1, -1, 2, -2) for b in (0, 1, -1)]
@@ -142,7 +150,14 @@
     lane8 = lax.broadcasted_iota(jnp.int32, (8, 128), 1)
     for copy in copies:
         copy.wait()
+    wait_bytes(rows_in.at[pl.ds(0, 5 * blocks)], rows_sem)
     lam = coupling[0]
+    center = 13 * blocks
+
+    def block_number(q, e):
+        used = e < counts[0, 0, 0, q]
+        return jnp.where(used, neighbours[0, 0, q, 0, e], 27 * blocks)
+
     leave_slots = jnp.full((8, 128), -1, jnp.int32)
     land_slots = jnp.full((8, 128), -1, jnp.int32)
     for m in range(16):
@@ -158,7 +173,7 @@
         sigma = jnp.where(hit, sigma_table[k], sigma)
         depth = jnp.where(hit, depth_table[k], depth)
         charge = jnp.where(hit, charge_table[k], charge)
-    flag = perts[0:blocks, :].astype(F32)
+    flag = kinds[blocks : 2 * blocks, :].astype(F32)
     table[0] = sigma * SIGMA_SCALE
     table[1] = jnp.sqrt(depth)
     table[2] = charge * CHARGE_SCALE
@@ -184,8 +199,8 @@
                 leaves[a, b] = pltpu.make_async_remote_copy(
                     leavers.at[LEAVE_CENTRE],
                     leavers.at[i],
-                    leave_send.at[i],
-                    leave_recv.at[i],
+                    ici_send,
+                    leave_recv,
                     along(-a, -b),
                     MESH,
                 )
@@ -195,8 +210,8 @@
         halos[a, b] = pltpu.make_async_remote_copy(
             raw.at[CENTRE],
             raw.at[i],
-            halo_send.at[i],
-            halo_recv.at[i],
+            ici_send,
+            halo_recv,
             along(-a, -b),
             MESH,
         )
@@ -214,129 +229,120 @@
     lane32 = lax.broadcasted_iota(jnp.int32, (32, 128), 1).astype(F32)
     step_x = jnp.where(row8 == 0, jnp.where(lane8 < 16, 1.0, -1.0), 0.0)
     ones8 = jnp.ones((8, 128), BF16)
-    seen = set()
-
-    def arrived(a, b):
-        if (a, b) != (0, 0) and (a, b) not in seen:
-            seen.add((a, b))
-            leaves[a, b].wait_recv()
-        return leavers.at[3 * (a + 2) + b + 1]
-
-    overs = []
-
-    def settle(a, b):
+    ghost[27 * blocks] = jnp.where(
+        row8 == 3, 1.0, jnp.where(row8 == 6, 0.15, jnp.where(row8 == 7, 1.0, 0.0))
+    )
+    itself = []
+    for q in range(blocks):
+        times = jnp.int32(0)
+        for e in range(listed):
+            times += jnp.where(block_number(q, e) == center + q, 1, 0)
+        itself.append(jnp.full((1, 128), times, jnp.int32).astype(F32))
+    around = ((0, 0), (0, 1), (0, -1), (-1, 0), (1, 0), (-1, 1), (1, 1), (-1, -1), (1, -1))
+    wait_bytes(leavers.at[pl.ds(0, len(leaves))], leave_recv)
+
+    for a, b in around:
         i = 3 * (a + 1) + b + 1
-        here, above, below = arrived(a, b), arrived(a + 1, b), arrived(a - 1, b)
-        if (a, b) != (0, 0):
-            halos[a, b].wait_recv()
-        slots = jnp.broadcast_to(here[...].T[0:32, 7:8], (32, 128))
-        tile = jnp.where(lane8 < 16, above[...], below[...]) + step_x
+        here, above, below = (leavers[3 * (a + 2 + k) + b + 1] for k in (0, 1, -1))
+        slots = jnp.broadcast_to(here.T[0:32, 7:8], (32, 128))
+        tile = jnp.where(lane8 < 16, above, below) + step_x
         tile = jnp.where(row8 == 7, pltpu.roll(tile, 1, 0), tile)
         parts = jnp.concatenate((*split3(tile), ones8), axis=0)
+        for q in range(blocks):
+            spread = (slots == lane32 + float(q * 128)).astype(F32).astype(BF16)
+            arrived = jnp.dot(parts[:, 0:32], spread, preferred_element_type=F32)
+            landed[i, q, 0:8] = join3(arrived)
+            landed[i, q, 8:16] = arrived[24:32]
+
+    wait_bytes(raw.at[pl.ds(0, len(halos))], halo_recv)
+    for a, b in around:
+        i = 3 * (a + 1) + b + 1
         offset = base
         for k, value in enumerate((a, b)):
             if value:
                 offset = jnp.where(row8 == k, scale * float(value), offset)
         for q in range(blocks):
-            spread = (slots == lane32 + float(q * 128)).astype(F32).astype(BF16)
-            landed = jnp.dot(parts[:, 0:32], spread, preferred_element_type=F32)
-            moved = jnp.where(landed[24:32] > 0.5, join3(landed), raw[i, q])
+            moved = jnp.where(landed[i, q, 8:16] > 0.5, landed[i, q, 0:8], raw[i, q])
             ghost[(3 * i + 1) * blocks + q] = moved * scale + offset
         over = pltpu.make_async_remote_copy(
             ghost.at[pl.ds((3 * i + 1) * blocks, blocks)],
             theirs.at[i],
-            over_send.at[i],
-            over_recv.at[i],
+            ici_send,
+            over_recv,
             along(0, 0, 1),
             MESH,
         )
         over.start()
-        overs.append((i, over))
-
-    ghost[27 * blocks] = jnp.where(
-        row8 == 3, 1.0, jnp.where(row8 == 6, 0.15, jnp.where(row8 == 7, 1.0, 0.0))
-    )
-    settle(0, 0)
-    center = 13 * blocks
+
+    pl.semaphore_wait(token.at[0], 2)
+    for a in (-4, 4):
+        signal(token.at[1], along(a, 0))
+    self_sums = [jnp.zeros((1, 128), F32)] * 3
     for q in range(blocks):
-        columns = ghost[center + q].T
+        tile = ghost[center + q]
+        columns = tile.T
         for k in range(8):
             own[k, q * 128 : q * 128 + 128, :] = jnp.broadcast_to(
                 columns[:, k : k + 1], (128, 128)
             )
-
-    def block_number(q, e):
-        used = e < counts[0, 0, 0, q]
-        return jnp.where(used, neighbours[0, 0, q, 0, e], 27 * blocks)
-
-    self_sums = [jnp.zeros((1, 128), F32)] * 3
-    for q in range(blocks):
-        itself = jnp.float32(0.0)
-        for e in range(listed):
-            itself += jnp.where(block_number(q, e) == center + q, 1.0, 0.0)
-        tile = ghost[center + q]
         atom = [tile[r : r + 1] for r in range(8)]
         _, _, _, _, u, root, t, ty, coul = pair(atom, atom)
         v = (ty - t) + coul
         g = u * ty + 0.25 * (coul * (root * root))
         off = 1.0 - atom[7]
         self_sums = [
-            total + itself * term for total, term in zip(self_sums, (v, off * v, off * g))
+            total + itself[q] * term for total, term in zip(self_sums, (v, off * v, off * g))
         ]
 
-    for b in (0, 1, -1):
-        settle(-1, b)
-    pl.semaphore_wait(token.at[0], 2)
-    for a in (-4, 4):
-        signal(token.at[1], along(a, 0))
-    for a, b in ((0, 1), (0, -1), (1, 0), (1, 1), (1, -1)):
-        settle(a, b)
-    for i, over in overs:
-        over.wait_recv()
+    wait_bytes(theirs, over_recv)
+    for i in range(9):
         for q in range(blocks):
             for c in (-1, 1):
                 ghost[(3 * i + 1 + c) * blocks + q] = theirs[i, q] + (step_z * float(c))
-    for copy in (*leaves.values(), *halos.values()):
-        copy.wait_send()
-    for _, over in overs:
-        over.wait_send()
 
     steps = blocks * 128 // CHUNK
     per_block = 128 // CHUNK
     halves = CHUNK // 8
 
-    def pair_step(k, sums):
-        q = k // per_block
-        atoms = [
-            [own[r, pl.ds(k * CHUNK + 8 * half, 8), :] for r in range(8)] for half in range(halves)
-        ]
-        v_sum, ov_sum, og_sum = sums
-        force = [[jnp.zeros((8, 128), F32)] * 3 for _ in atoms]
-        for e in range(listed):
-            number = block_number(q, e)
-            other = [ghost[number, r : r + 1, :] for r in range(8)]
-            for half, atom in enumerate(atoms):
-                d, _, r4, inverse, u, root, t, ty, coul = pair(atom, other)
-                w = jnp.minimum(atom[7], other[7])
-                off = 1.0 - w
-                v = (ty - t) + coul
-                m = coul * (root * root)
-                g = u * ty + 0.25 * m
-                v_sum, ov_sum, og_sum = v_sum + v, ov_sum + off * v, og_sum + off * g
-                f = ((r4 * inverse) * ty + m * (1.0 / 12.0)) * w
-                force[half] = [total + f * part for total, part in zip(force[half], d)]
-        for half, totals in enumerate(force):
-            for axis, total in enumerate(totals):
-                force_acc[axis, pl.ds(k * CHUNK + 8 * half, 8), :] = total
-        return v_sum, ov_sum, og_sum
+    def pair_step(with_energy, with_force):
+        def step(k, sums):
+            q = k // per_block
+            atoms = [
+                [own[r, pl.ds(k * CHUNK + 8 * half, 8), :] for r in range(8)]
+                for half in range(halves)
+            ]
+            force = [[jnp.zeros((8, 128), F32)] * 3 for _ in atoms]
+            for e in range(listed):
+                number = block_number(q, e)
+                other = [ghost[number, r : r + 1, :] for r in range(8)]
+                for half, atom in enumerate(atoms):
+                    d, _, r4, inverse, u, root, t, ty, coul = pair(atom, other)
+                    w = jnp.minimum(atom[7], other[7])
+                    m = coul * (root * root)
+                    if with_energy:
+                        v_sum, ov_sum, og_sum = sums
+                        off = 1.0 - w
+                        v = (ty - t) + coul
+                        g = u * ty + 0.25 * m
+                        sums = v_sum + v, ov_sum + off * v, og_sum + off * g
+                    if with_force:
+                        f = ((r4 * inverse) * ty + m * (1.0 / 12.0)) * w
+                        force[half] = [total + f * part for total, part in zip(force[half], d)]
+            if with_force:
+                for half, totals in enumerate(force):
+                    for axis, total in enumerate(totals):
+                        force_acc[axis, pl.ds(k * CHUNK + 8 * half, 8), :] = total
+            return sums
+
+        return step
 
     zero = jnp.zeros((8, 128), F32)
-    third = steps // 3
-    sums = lax.fori_loop(0, third, pair_step, (zero, zero, zero))
+    both = steps - LATE_A - LATE_B
+    sums = lax.fori_loop(0, both, pair_step(True, True), (zero, zero, zero))
     pl.semaphore_wait(token.at[1], 2)
     for a in (-8, 8):
         signal(token.at[2], along(a, 0))
-    sums = lax.fori_loop(third, steps, pair_step, sums)
+    sums = lax.fori_loop(both, steps, pair_step(True, False), sums)
     v_row, ov_row, og_row = (
         jnp.sum(total, axis=0, keepdims=True) - itself for total, itself in zip(sums, self_sums)
     )
@@ -355,8 +361,8 @@
             pltpu.make_async_remote_copy(
                 plane_sums.at[my_peer],
                 plane_sums.at[my_peer],
-                plane_send.at[i],
-                plane_recv.at[i],
+                plane_send,
+                plane_recv,
                 along(0, b, c),
                 MESH,
             )
@@ -364,6 +370,7 @@
     for copy in plane_copies:
         copy.start()
 
+    lax.fori_loop(both, both + LATE_A, pair_step(False, True), ())
     ones = jnp.ones((8, 384), BF16)
 
     def row_sums(axis):
@@ -376,10 +383,7 @@
             )
             forces_out[axis, 0, 0, :, q * 128 : q * 128 + 128] = total[0:1] * FORCE_SCALE
 
-    row_sums(0)
-    row_sums(1)
-    for copy in plane_copies:
-        copy.wait()
+    wait_bytes(plane_sums.at[pl.ds(0, len(peers))], plane_recv)
     total = plane_sums[0]
     for i in range(1, n_dy * n_dz):
         total = total + plane_sums[i]
@@ -391,23 +395,35 @@
             pltpu.make_async_remote_copy(
                 line_sums.at[me_x],
                 line_sums.at[me_x],
-                line_send.at[d],
-                line_recv.at[d],
+                line_send,
+                line_recv,
                 along(d, 0),
                 MESH,
             )
         )
     for copy in line_copies:
         copy.start()
-    row_sums(2)
-    for copy in line_copies:
-        copy.wait()
+    lax.fori_loop(both + LATE_A, steps, pair_step(False, True), ())
+    for axis in range(3):
+        row_sums(axis)
+    wait_bytes(line_sums.at[pl.ds(0, n_dx - 1)], line_recv)
     total = line_sums[0]
     for i in range(1, n_dx):
         total = total + line_sums[i]
     norm = 0.5 / (blocks * 128 * n_dx * n_dy * n_dz)
     energy_out[0] = jnp.sum(jnp.where(lane1 < 64, total, 0.0)) * norm
     dhdl_out[0] = jnp.sum(jnp.where(lane1 < 64, 0.0, total)) * (-norm / lam)
+    results = [
+        pltpu.make_async_copy(energy_out, energy_hbm, out_sem.at[0]),
+        pltpu.make_async_copy(dhdl_out, dhdl_hbm, out_sem.at[1]),
+    ]
+    for copy in results:
+        copy.start()
+    wait_bytes(ghost.at[pl.ds(0, len(leaves) + (len(halos) + 9) * blocks)], ici_send)
+    wait_bytes(plane_sums.at[pl.ds(0, len(peers))], plane_send)
+    wait_bytes(line_sums.at[pl.ds(0, n_dx - 1)], line_send)
+    for copy in results:
+        copy.wait()
 
 
 def on_device(
@@ -429,7 +445,6 @@
     sizes = (n_dx, n_dy, n_dz, blocks, neighbours.shape[-1])
     neighbours = neighbours.transpose(0, 1, 3, 2, 4)
     hbm = pl.BlockSpec(memory_space=pltpu.HBM)
-    smem = pl.BlockSpec(memory_space=pltpu.SMEM)
     dma, regular = pltpu.SemaphoreType.DMA, pltpu.SemaphoreType.REGULAR
     scalars = (
         leaving,
@@ -444,36 +459,31 @@
     return pl.pallas_call(
         lambda *refs: kernel(sizes, *refs),
         out_shape=(
-            jax.ShapeDtypeStruct(fraction.shape, F32),
+            pltpu.VMEM(fraction.shape, F32),
             jax.ShapeDtypeStruct((1,), F32),
             jax.ShapeDtypeStruct((1,), F32),
         ),
         in_specs=[hbm] * 11,
-        out_specs=(pl.BlockSpec(memory_space=pltpu.VMEM), smem, smem),
+        out_specs=(pl.BlockSpec(memory_space=pltpu.VMEM), hbm, hbm),
         scratch_shapes=[
+            pltpu.SMEM((1,), F32),
+            pltpu.SMEM((1,), F32),
             *[pltpu.SMEM(array.shape, array.dtype) for array in scalars],
-            pltpu.VMEM((8, 128), jnp.int32),
-            pltpu.VMEM((8, 128), jnp.int32),
+            pltpu.VMEM((2 * blocks, 128), jnp.int32),
+            pltpu.VMEM((5 * blocks, 128), F32),
             pltpu.VMEM((4, blocks, 128), F32),
             pltpu.VMEM((9, blocks, 8, 128), F32),
             pltpu.VMEM((15, 8, 128), F32),
+            pltpu.VMEM((9, blocks, 16, 128), F32),
             pltpu.VMEM((9, blocks, 8, 128), F32),
             pltpu.VMEM((27 * blocks + 1, 8, 128), F32),
             pltpu.VMEM((8, atoms, 128), F32),
             pltpu.VMEM((3, atoms, 128), F32),
             pltpu.VMEM((n_dy * n_dz, 1, 128), F32),
             pltpu.VMEM((n_dx, 1, 128), F32),
-            dma((8 + 5 * blocks,)),
-            dma((15,)),
-            dma((15,)),
-            dma((9,)),
-            dma((9,)),
-            dma((9,)),
-            dma((9,)),
-            dma((n_dy * n_dz,)),
-            dma((n_dy * n_dz,)),
-            dma((n_dx,)),
-            dma((n_dx,)),
+            dma((len(scalars),)),
+            *[dma] * 9,
+            dma((2,)),
             regular((3,)),
         ],
         compiler_params=pltpu.CompilerParams(

time: 83.2 us -> 80 us (0.962)
  Pallas kernels: 76.7 us -> 74.4 us
    pallas_call x1, Pallas kernels: 76.7 us -> 74.4 us  [on_device(): pl.pallas_call(lambda *refs: kernel(sizes, *refs), out_shape=(pltpu.VMEM(...]
where the time goes in v3:
time: 80 us; the launch traced here: 79.7 us
  Pallas kernels  74.4 us (93%)
  between operations  4.74 us (6%)
    pallas_call x1, Pallas kernels, on_device(): pl.pallas_call(lambda *refs: kernel(sizes, *refs), out_shape=(pltpu.VMEM(...  74.4 us

profile of v3, /device:TPU:33, one launch (start us, length us, event | category | flops | bytes accessed | tf_op | source)
XLA Modules:
  0.0 79.7 jit_solution(1164162964123656072)
XLA Ops:
  1.3 74.4 %step.1 = (f32[3,1,1,1,768]{4,3,2,1,0:T(1,128)S(1)}, f32[1]{0:T(128)}, f32[1]{0:T(128)}) custom-call(f32[3,1,1,1,768]{4,3,2,1,0:T(1,128)} %refs_0_.1, s32[1,1,1,768]{3,2,1,0:T(1,128)} %refs_1_.1, s32[1,1,1,768]{3,2,1,0:T(1,128)} %refs_2_.1, s32[1,1,1,2,16]{4,3,2,1,0:T(2,128)} %refs_3_.1, s32[1,1,6,1,16]{4,3,2,1,0:T(1,128)} %bitcast.1, ...), custom_call_target="tpu_custom_call" | custom-call | tf_op jit(solution)/shard_map/step/pallas_call | solution.py:459
  75.6 0.6 copy.17

commit v4 on v3

--- a/solution.py
+++ b/solution.py
@@ -83,10 +83,13 @@
     landed,
     theirs,
     ghost,
+    places,
     own,
     force_acc,
     plane_sums,
     line_sums,
+    total_out,
+    total_in,
     in_sem,
     rows_sem,
     ici_send,
@@ -97,6 +100,8 @@
     plane_recv,
     line_send,
     line_recv,
+    total_send,
+    total_recv,
     out_sem,
     token,
 ):
@@ -152,11 +157,8 @@
         copy.wait()
     wait_bytes(rows_in.at[pl.ds(0, 5 * blocks)], rows_sem)
     lam = coupling[0]
-    center = 13 * blocks
-
-    def block_number(q, e):
-        used = e < counts[0, 0, 0, q]
-        return jnp.where(used, neighbours[0, 0, q, 0, e], 27 * blocks)
+    plane = 9 * blocks
+    center = plane + CENTRE * blocks
 
     leave_slots = jnp.full((8, 128), -1, jnp.int32)
     land_slots = jnp.full((8, 128), -1, jnp.int32)
@@ -236,9 +238,17 @@
     for q in range(blocks):
         times = jnp.int32(0)
         for e in range(listed):
-            times += jnp.where(block_number(q, e) == center + q, 1, 0)
+            number = neighbours[0, 0, q, 0, e]
+            domain = number // blocks
+            where = (domain % 3) * plane + (domain // 3) * blocks + number % blocks
+            where = jnp.where(e < counts[0, 0, 0, q], where, 3 * plane)
+            places[q * listed + e] = where
+            times += jnp.where(where == center + q, 1, 0)
         itself.append(jnp.full((1, 128), times, jnp.int32).astype(F32))
     around = ((0, 0), (0, 1), (0, -1), (-1, 0), (1, 0), (-1, 1), (1, 1), (-1, -1), (1, -1))
+    pl.semaphore_wait(token.at[0], 2)
+    for a in (-4, 4):
+        signal(token.at[1], along(a, 0))
     wait_bytes(leavers.at[pl.ds(0, len(leaves))], leave_recv)
 
     for a, b in around:
@@ -263,20 +273,10 @@
                 offset = jnp.where(row8 == k, scale * float(value), offset)
         for q in range(blocks):
             moved = jnp.where(landed[i, q, 8:16] > 0.5, landed[i, q, 0:8], raw[i, q])
-            ghost[(3 * i + 1) * blocks + q] = moved * scale + offset
-        over = pltpu.make_async_remote_copy(
-            ghost.at[pl.ds((3 * i + 1) * blocks, blocks)],
-            theirs.at[i],
-            ici_send,
-            over_recv,
-            along(0, 0, 1),
-            MESH,
-        )
-        over.start()
-
-    pl.semaphore_wait(token.at[0], 2)
-    for a in (-4, 4):
-        signal(token.at[1], along(a, 0))
+            ghost[plane + i * blocks + q] = moved * scale + offset
+    pltpu.make_async_remote_copy(
+        ghost.at[pl.ds(plane, plane)], theirs, ici_send, over_recv, along(0, 0, 1), MESH
+    ).start()
     self_sums = [jnp.zeros((1, 128), F32)] * 3
     for q in range(blocks):
         tile = ghost[center + q]
@@ -295,10 +295,10 @@
         ]
 
     wait_bytes(theirs, over_recv)
-    for i in range(9):
-        for q in range(blocks):
-            for c in (-1, 1):
-                ghost[(3 * i + 1 + c) * blocks + q] = theirs[i, q] + (step_z * float(c))
+    for i in range(plane):
+        tile = theirs[i]
+        ghost[i] = tile - step_z
+        ghost[2 * plane + i] = tile + step_z
 
     steps = blocks * 128 // CHUNK
     per_block = 128 // CHUNK
@@ -313,8 +313,8 @@
             ]
             force = [[jnp.zeros((8, 128), F32)] * 3 for _ in atoms]
             for e in range(listed):
-                number = block_number(q, e)
-                other = [ghost[number, r : r + 1, :] for r in range(8)]
+                place = places[q * listed + e]
+                other = [ghost[place, r : r + 1, :] for r in range(8)]
                 for half, atom in enumerate(atoms):
                     d, _, r4, inverse, u, root, t, ty, coul = pair(atom, other)
                     w = jnp.minimum(atom[7], other[7])
@@ -353,22 +353,29 @@
     dhdl_row += pltpu.roll(dhdl_row, 64, 1)
     part = jnp.where(lane1 < 64, energy_row, dhdl_row)
 
+    leader = me_z == n_dz - 1
     my_peer = me_y * n_dz + me_z
     plane_sums[my_peer] = part
-    plane_copies = []
-    for i, (b, c) in enumerate(peers):
-        plane_copies.append(
-            pltpu.make_async_remote_copy(
-                plane_sums.at[my_peer],
-                plane_sums.at[my_peer],
-                plane_send,
-                plane_recv,
-                along(0, b, c),
-                MESH,
-            )
-        )
-    for copy in plane_copies:
-        copy.start()
+
+    def send_part(b, c):
+        pltpu.make_async_remote_copy(
+            plane_sums.at[my_peer],
+            plane_sums.at[my_peer],
+            plane_send,
+            plane_recv,
+            along(0, b, c),
+            MESH,
+        ).start()
+
+    @pl.when(jnp.logical_not(leader))
+    def _():
+        for b in (0, 1, -1, 2):
+            send_part(b, 1)
+
+    @pl.when(leader)
+    def _():
+        for b in (1, -1, 2):
+            send_part(b, 0)
 
     lax.fori_loop(both, both + LATE_A, pair_step(False, True), ())
     ones = jnp.ones((8, 384), BF16)
@@ -383,15 +390,15 @@
             )
             forces_out[axis, 0, 0, :, q * 128 : q * 128 + 128] = total[0:1] * FORCE_SCALE
 
-    wait_bytes(plane_sums.at[pl.ds(0, len(peers))], plane_recv)
-    total = plane_sums[0]
-    for i in range(1, n_dy * n_dz):
-        total = total + plane_sums[i]
-    line_sums[me_x] = total
-    pl.semaphore_wait(token.at[2], 2)
-    line_copies = []
-    for d in sorted(range(1, n_dx), key=lambda d: min(d, n_dx - d)):
-        line_copies.append(
+    @pl.when(leader)
+    def _():
+        wait_bytes(plane_sums.at[pl.ds(0, len(peers))], plane_recv)
+        total = plane_sums[0]
+        for i in range(1, n_dy * n_dz):
+            total = total + plane_sums[i]
+        line_sums[me_x] = total
+        pl.semaphore_wait(token.at[2], 2)
+        for d in sorted(range(1, n_dx), key=lambda d: min(d, n_dx - d)):
             pltpu.make_async_remote_copy(
                 line_sums.at[me_x],
                 line_sums.at[me_x],
@@ -399,17 +406,32 @@
                 line_recv,
                 along(d, 0),
                 MESH,
-            )
-        )
-    for copy in line_copies:
-        copy.start()
+            ).start()
+
+    @pl.when(jnp.logical_not(leader))
+    def _():
+        pl.semaphore_wait(token.at[2], 2)
+
     lax.fori_loop(both + LATE_A, steps, pair_step(False, True), ())
     for axis in range(3):
         row_sums(axis)
-    wait_bytes(line_sums.at[pl.ds(0, n_dx - 1)], line_recv)
-    total = line_sums[0]
-    for i in range(1, n_dx):
-        total = total + line_sums[i]
+    @pl.when(leader)
+    def _():
+        wait_bytes(line_sums.at[pl.ds(0, n_dx - 1)], line_recv)
+        total = line_sums[0]
+        for i in range(1, n_dx):
+            total = total + line_sums[i]
+        total_out[...] = total
+        pltpu.make_async_remote_copy(
+            total_out, total_in, total_send, total_recv, along(0, 0, 1), MESH
+        ).start()
+
+    @pl.when(jnp.logical_not(leader))
+    def _():
+        wait_bytes(total_in, total_recv)
+        total_out[...] = total_in[...]
+
+    total = total_out[...]
     norm = 0.5 / (blocks * 128 * n_dx * n_dy * n_dz)
     energy_out[0] = jnp.sum(jnp.where(lane1 < 64, total, 0.0)) * norm
     dhdl_out[0] = jnp.sum(jnp.where(lane1 < 64, 0.0, total)) * (-norm / lam)
@@ -420,8 +442,17 @@
     for copy in results:
         copy.start()
     wait_bytes(ghost.at[pl.ds(0, len(leaves) + (len(halos) + 9) * blocks)], ici_send)
-    wait_bytes(plane_sums.at[pl.ds(0, len(peers))], plane_send)
-    wait_bytes(line_sums.at[pl.ds(0, n_dx - 1)], line_send)
+
+    @pl.when(leader)
+    def _():
+        wait_bytes(plane_sums.at[pl.ds(0, n_dy - 1)], plane_send)
+        wait_bytes(line_sums.at[pl.ds(0, n_dx - 1)], line_send)
+        wait_bytes(total_out, total_send)
+
+    @pl.when(jnp.logical_not(leader))
+    def _():
+        wait_bytes(plane_sums.at[pl.ds(0, n_dy)], plane_send)
+
     for copy in results:
         copy.wait()
 
@@ -475,14 +506,17 @@
             pltpu.VMEM((9, blocks, 8, 128), F32),
             pltpu.VMEM((15, 8, 128), F32),
             pltpu.VMEM((9, blocks, 16, 128), F32),
-            pltpu.VMEM((9, blocks, 8, 128), F32),
+            pltpu.VMEM((9 * blocks, 8, 128), F32),
             pltpu.VMEM((27 * blocks + 1, 8, 128), F32),
+            pltpu.SMEM((blocks * neighbours.shape[-1],), jnp.int32),
             pltpu.VMEM((8, atoms, 128), F32),
             pltpu.VMEM((3, atoms, 128), F32),
             pltpu.VMEM((n_dy * n_dz, 1, 128), F32),
             pltpu.VMEM((n_dx, 1, 128), F32),
+            pltpu.VMEM((1, 128), F32),
+            pltpu.VMEM((1, 128), F32),
             dma((len(scalars),)),
-            *[dma] * 9,
+            *[dma] * 11,
             dma((2,)),
             regular((3,)),
         ],

time: 80 us -> 79.1 us (0.989)
  Pallas kernels: 74.4 us -> 73.5 us
    pallas_call x1, Pallas kernels: 74.4 us -> 73.5 us  [on_device(): pl.pallas_call(lambda *refs: kernel(sizes, *refs), out_shape=(pltpu.VMEM(...]
where the time goes in v4:
time: 79.1 us; the launch traced here: 78.9 us
  Pallas kernels  73.5 us (93%)
  between operations  4.74 us (6%)
    pallas_call x1, Pallas kernels, on_device(): pl.pallas_call(lambda *refs: kernel(sizes, *refs), out_shape=(pltpu.VMEM(...  73.5 us

profile of v4, /device:TPU:33, one launch (start us, length us, event | category | flops | bytes accessed | tf_op | source)
XLA Modules:
  0.0 78.9 jit_solution(11102250060274066767)
XLA Ops:
  1.3 73.5 %step.1 = (f32[3,1,1,1,768]{4,3,2,1,0:T(1,128)S(1)}, f32[1]{0:T(128)}, f32[1]{0:T(128)}) custom-call(f32[3,1,1,1,768]{4,3,2,1,0:T(1,128)} %refs_0_.1, s32[1,1,1,768]{3,2,1,0:T(1,128)} %refs_1_.1, s32[1,1,1,768]{3,2,1,0:T(1,128)} %refs_2_.1, s32[1,1,1,2,16]{4,3,2,1,0:T(2,128)} %refs_3_.1, s32[1,1,6,1,16]{4,3,2,1,0:T(1,128)} %bitcast.1, ...), custom_call_target="tpu_custom_call" | custom-call | tf_op jit(solution)/shard_map/step/pallas_call | solution.py:490
  74.8 0.6 copy.17

commit v5 on v4

--- a/solution.py
+++ b/solution.py
@@ -17,7 +17,8 @@
 CENTRE = 4
 LEAVE_CENTRE = 7
 CHUNK = 16
-LATE_A, LATE_B = 14, 20
+WIDE = 32
+LATE_A, LATE_B = 18, 18
 
 
 def split3(x):
@@ -145,7 +146,7 @@
         pltpu.make_async_copy(ref, ref, semaphore).wait()
 
     peers = [(b, c) for b in range(n_dy) for c in range(n_dz) if (b, c) != (0, 0)]
-    near = [(a, b, 0) for a in (1, -1, 2, -2) for b in (0, 1, -1)]
+    near = [(a, b, 0) for a in (2, -2, 1, -1) for b in (1, -1, 0)]
     near += [(0, b, c) for b, c in peers]
     barrier = pltpu.get_barrier_semaphore()
     for device in near:
@@ -194,8 +195,8 @@
 
     pl.semaphore_wait(barrier, len(near))
     leaves, halos = {}, {}
-    for a in (1, -1, 2, -2, 0):
-        for b in (0, 1, -1):
+    for a in (2, -2, 1, -1, 0):
+        for b in (1, -1, 0):
             if (a, b) != (0, 0):
                 i = 3 * (a + 2) + b + 1
                 leaves[a, b] = pltpu.make_async_remote_copy(
@@ -225,15 +226,13 @@
     scale = jnp.ones((8, 128), F32)
     for k in range(3):
         scale = jnp.where(row8 == k, edge[k] * spacing, scale)
-    scale = jnp.where(row8 == 6, 0.25 * lam, jnp.where(row8 == 7, -lam, scale))
-    base = jnp.where(row8 == 6, 0.15, jnp.where(row8 == 7, 1.0, 0.0))
+    scale = jnp.where(row8 == 6, 0.25 * lam, jnp.where(row8 == 7, lam, scale))
+    base = jnp.where(row8 == 6, 0.15, 0.0)
     step_z = jnp.where(row8 == 2, scale, 0.0)
     lane32 = lax.broadcasted_iota(jnp.int32, (32, 128), 1).astype(F32)
     step_x = jnp.where(row8 == 0, jnp.where(lane8 < 16, 1.0, -1.0), 0.0)
     ones8 = jnp.ones((8, 128), BF16)
-    ghost[27 * blocks] = jnp.where(
-        row8 == 3, 1.0, jnp.where(row8 == 6, 0.15, jnp.where(row8 == 7, 1.0, 0.0))
-    )
+    ghost[27 * blocks] = jnp.where(row8 == 3, 1.0, jnp.where(row8 == 6, 0.15, 0.0))
     itself = []
     for q in range(blocks):
         times = jnp.int32(0)
@@ -258,11 +257,18 @@
         tile = jnp.where(lane8 < 16, above, below) + step_x
         tile = jnp.where(row8 == 7, pltpu.roll(tile, 1, 0), tile)
         parts = jnp.concatenate((*split3(tile), ones8), axis=0)
+        spread = jnp.concatenate(
+            [
+                (slots == lane32 + float(q * 128)).astype(F32).astype(BF16)
+                for q in range(blocks)
+            ],
+            axis=1,
+        )
+        arrived = jnp.dot(parts[:, 0:32], spread, preferred_element_type=F32)
+        rows_new = join3(arrived)
         for q in range(blocks):
-            spread = (slots == lane32 + float(q * 128)).astype(F32).astype(BF16)
-            arrived = jnp.dot(parts[:, 0:32], spread, preferred_element_type=F32)
-            landed[i, q, 0:8] = join3(arrived)
-            landed[i, q, 8:16] = arrived[24:32]
+            landed[i, q, 0:8] = rows_new[:, q * 128 : q * 128 + 128]
+            landed[i, q, 8:16] = arrived[24:32, q * 128 : q * 128 + 128]
 
     wait_bytes(raw.at[pl.ds(0, len(halos))], halo_recv)
     for a, b in around:
@@ -289,7 +295,7 @@
         _, _, _, _, u, root, t, ty, coul = pair(atom, atom)
         v = (ty - t) + coul
         g = u * ty + 0.25 * (coul * (root * root))
-        off = 1.0 - atom[7]
+        off = atom[7]
         self_sums = [
             total + itself[q] * term for total, term in zip(self_sums, (v, off * v, off * g))
         ]
@@ -301,14 +307,14 @@
         ghost[2 * plane + i] = tile + step_z
 
     steps = blocks * 128 // CHUNK
-    per_block = 128 // CHUNK
-    halves = CHUNK // 8
-
-    def pair_step(with_energy, with_force):
+
+    def pair_step(with_energy, with_force, chunk=CHUNK):
+        halves = chunk // 8
+
         def step(k, sums):
-            q = k // per_block
+            q = k // (128 // chunk)
             atoms = [
-                [own[r, pl.ds(k * CHUNK + 8 * half, 8), :] for r in range(8)]
+                [own[r, pl.ds(k * chunk + 8 * half, 8), :] for r in range(8)]
                 for half in range(halves)
             ]
             force = [[jnp.zeros((8, 128), F32)] * 3 for _ in atoms]
@@ -317,21 +323,20 @@
                 other = [ghost[place, r : r + 1, :] for r in range(8)]
                 for half, atom in enumerate(atoms):
                     d, _, r4, inverse, u, root, t, ty, coul = pair(atom, other)
-                    w = jnp.minimum(atom[7], other[7])
+                    off = jnp.maximum(atom[7], other[7])
                     m = coul * (root * root)
                     if with_energy:
                         v_sum, ov_sum, og_sum = sums
-                        off = 1.0 - w
                         v = (ty - t) + coul
                         g = u * ty + 0.25 * m
                         sums = v_sum + v, ov_sum + off * v, og_sum + off * g
                     if with_force:
-                        f = ((r4 * inverse) * ty + m * (1.0 / 12.0)) * w
+                        f = ((r4 * inverse) * ty + m * (1.0 / 12.0)) * (1.0 - off)
                         force[half] = [total + f * part for total, part in zip(force[half], d)]
             if with_force:
                 for half, totals in enumerate(force):
                     for axis, total in enumerate(totals):
-                        force_acc[axis, pl.ds(k * CHUNK + 8 * half, 8), :] = total
+                        force_acc[axis, pl.ds(k * chunk + 8 * half, 8), :] = total
             return sums
 
         return step
@@ -342,7 +347,8 @@
     pl.semaphore_wait(token.at[1], 2)
     for a in (-8, 8):
         signal(token.at[2], along(a, 0))
-    sums = lax.fori_loop(both, steps, pair_step(True, False), sums)
+    wide = WIDE // CHUNK
+    sums = lax.fori_loop(both // wide, steps // wide, pair_step(True, False, WIDE), sums)
     v_row, ov_row, og_row = (
         jnp.sum(total, axis=0, keepdims=True) - itself for total, itself in zip(sums, self_sums)
     )

time: 79.1 us -> 78.5 us (level)
  no operation moved by 1% of the time
where the time goes in v5:
time: 78.5 us; the launch traced here: 78.3 us
  Pallas kernels  72.9 us (93%)
  between operations  4.74 us (6%)
    pallas_call x1, Pallas kernels, on_device(): pl.pallas_call(lambda *refs: kernel(sizes, *refs), out_shape=(pltpu.VMEM(...  72.9 us

profile of v5, /device:TPU:33, one launch (start us, length us, event | category | flops | bytes accessed | tf_op | source)
XLA Modules:
  0.0 78.3 jit_solution(2400706531097088753)
XLA Ops:
  1.3 72.9 %step.1 = (f32[3,1,1,1,768]{4,3,2,1,0:T(1,128)S(1)}, f32[1]{0:T(128)}, f32[1]{0:T(128)}) custom-call(f32[3,1,1,1,768]{4,3,2,1,0:T(1,128)} %refs_0_.1, s32[1,1,1,768]{3,2,1,0:T(1,128)} %refs_1_.1, s32[1,1,1,768]{3,2,1,0:T(1,128)} %refs_2_.1, s32[1,1,1,2,16]{4,3,2,1,0:T(2,128)} %refs_3_.1, s32[1,1,6,1,16]{4,3,2,1,0:T(1,128)} %bitcast.1, ...), custom_call_target="tpu_custom_call" | custom-call | tf_op jit(solution)/shard_map/step/pallas_call | solution.py:496
  74.2 0.6 copy.17

commit v6 on v5

--- a/solution.py
+++ b/solution.py
@@ -81,6 +81,7 @@
     table,
     raw,
     leavers,
+    came,
     landed,
     theirs,
     ghost,
@@ -94,6 +95,7 @@
     in_sem,
     rows_sem,
     ici_send,
+    leave_send,
     leave_recv,
     halo_recv,
     over_recv,
@@ -161,12 +163,13 @@
     plane = 9 * blocks
     center = plane + CENTRE * blocks
 
-    leave_slots = jnp.full((8, 128), -1, jnp.int32)
-    land_slots = jnp.full((8, 128), -1, jnp.int32)
+    lane32 = jnp.bitwise_and(lane8, 31)
+    leave_slots = jnp.zeros((8, 128), jnp.int32)
+    land_slots = jnp.zeros((8, 128), jnp.int32)
     for m in range(16):
         up, down = leaving[0, 0, 0, 0, m], leaving[0, 0, 0, 1, m]
-        leave_slots = jnp.where(lane8 == m, down, jnp.where(lane8 == m + 16, up, leave_slots))
-        land_slots = jnp.where(lane8 == m, up, jnp.where(lane8 == m + 16, down, land_slots))
+        leave_slots = jnp.where(lane32 == m, down, jnp.where(lane32 == m + 16, up, leave_slots))
+        land_slots = jnp.where(lane32 == m, up, jnp.where(lane32 == m + 16, down, land_slots))
     kind = kinds[0:blocks, :]
     sigma = jnp.zeros((blocks, 128), F32)
     depth = jnp.zeros((blocks, 128), F32)
@@ -191,7 +194,13 @@
         pick = (leave_slots[0:1] == rows + q * 128).astype(F32).astype(BF16)
         parts = jnp.concatenate(split3(raw[CENTRE, q]), axis=0)
         gathered += jnp.dot(parts, pick, preferred_element_type=F32)
-    leavers[LEAVE_CENTRE] = jnp.where(row8 == 7, land_slots.astype(F32), join3(gathered))
+    going = jnp.where(row8 == 7, land_slots.astype(F32), join3(gathered))
+    quarter = lax.broadcasted_iota(jnp.int32, (1, 128), 1) // 32
+    for half in range(2):
+        line = going[4 * half : 4 * half + 1]
+        for k in range(1, 4):
+            line = jnp.where(quarter == k, going[4 * half + k : 4 * half + k + 1], line)
+        leavers[LEAVE_CENTRE, half : half + 1, :] = line
 
     pl.semaphore_wait(barrier, len(near))
     leaves, halos = {}, {}
@@ -202,7 +211,7 @@
                 leaves[a, b] = pltpu.make_async_remote_copy(
                     leavers.at[LEAVE_CENTRE],
                     leavers.at[i],
-                    ici_send,
+                    leave_send,
                     leave_recv,
                     along(-a, -b),
                     MESH,
@@ -250,10 +259,17 @@
         signal(token.at[1], along(a, 0))
     wait_bytes(leavers.at[pl.ds(0, len(leaves))], leave_recv)
 
+    for i in range(15):
+        packed = leavers[i]
+        for k in range(4):
+            lines = packed if k == 0 else pltpu.roll(packed, 128 - 32 * k, 1)
+            for half in range(2):
+                came[i, 4 * half + k : 4 * half + k + 1, :] = lines[half : half + 1]
+    places_in = jnp.concatenate([came[3 + i, 7:8, :] for i in range(9)], axis=0).T
     for a, b in around:
         i = 3 * (a + 1) + b + 1
-        here, above, below = (leavers[3 * (a + 2 + k) + b + 1] for k in (0, 1, -1))
-        slots = jnp.broadcast_to(here.T[0:32, 7:8], (32, 128))
+        above, below = (came[3 * (a + 2 + k) + b + 1] for k in (1, -1))
+        slots = jnp.broadcast_to(places_in[0:32, i : i + 1], (32, 128))
         tile = jnp.where(lane8 < 16, above, below) + step_x
         tile = jnp.where(row8 == 7, pltpu.roll(tile, 1, 0), tile)
         parts = jnp.concatenate((*split3(tile), ones8), axis=0)
@@ -284,12 +300,12 @@
         ghost.at[pl.ds(plane, plane)], theirs, ici_send, over_recv, along(0, 0, 1), MESH
     ).start()
     self_sums = [jnp.zeros((1, 128), F32)] * 3
+    columns = jnp.concatenate([ghost[center + q] for q in range(blocks)], axis=0).T
     for q in range(blocks):
         tile = ghost[center + q]
-        columns = tile.T
         for k in range(8):
             own[k, q * 128 : q * 128 + 128, :] = jnp.broadcast_to(
-                columns[:, k : k + 1], (128, 128)
+                columns[:, 8 * q + k : 8 * q + k + 1], (128, 128)
             )
         atom = [tile[r : r + 1] for r in range(8)]
         _, _, _, _, u, root, t, ty, coul = pair(atom, atom)
@@ -447,7 +463,8 @@
     ]
     for copy in results:
         copy.start()
-    wait_bytes(ghost.at[pl.ds(0, len(leaves) + (len(halos) + 9) * blocks)], ici_send)
+    wait_bytes(leavers.at[pl.ds(0, len(leaves))], leave_send)
+    wait_bytes(ghost.at[pl.ds(0, (len(halos) + 9) * blocks)], ici_send)
 
     @pl.when(leader)
     def _():
@@ -510,6 +527,7 @@
             pltpu.VMEM((5 * blocks, 128), F32),
             pltpu.VMEM((4, blocks, 128), F32),
             pltpu.VMEM((9, blocks, 8, 128), F32),
+            pltpu.VMEM((15, 2, 128), F32),
             pltpu.VMEM((15, 8, 128), F32),
             pltpu.VMEM((9, blocks, 16, 128), F32),
             pltpu.VMEM((9 * blocks, 8, 128), F32),
@@ -522,7 +540,7 @@
             pltpu.VMEM((1, 128), F32),
             pltpu.VMEM((1, 128), F32),
             dma((len(scalars),)),
-            *[dma] * 11,
+            *[dma] * 12,
             dma((2,)),
             regular((3,)),
         ],

time: 78.5 us -> 78.1 us (level)
  no operation moved by 1% of the time
where the time goes in v6:
time: 78.1 us; the launch traced here: 77.9 us
  Pallas kernels  72.5 us (93%)
  between operations  4.74 us (6%)
    pallas_call x1, Pallas kernels, on_device(): pl.pallas_call(lambda *refs: kernel(sizes, *refs), out_shape=(pltpu.VMEM(...  72.5 us

profile of v6, /device:TPU:33, one launch (start us, length us, event | category | flops | bytes accessed | tf_op | source)
XLA Modules:
  0.0 77.9 jit_solution(7543734283726149228)
XLA Ops:
  1.3 72.5 %step.1 = (f32[3,1,1,1,768]{4,3,2,1,0:T(1,128)S(1)}, f32[1]{0:T(128)}, f32[1]{0:T(128)}) custom-call(f32[3,1,1,1,768]{4,3,2,1,0:T(1,128)} %refs_0_.1, s32[1,1,1,768]{3,2,1,0:T(1,128)} %refs_1_.1, s32[1,1,1,768]{3,2,1,0:T(1,128)} %refs_2_.1, s32[1,1,1,2,16]{4,3,2,1,0:T(2,128)} %refs_3_.1, s32[1,1,6,1,16]{4,3,2,1,0:T(1,128)} %bitcast.1, ...), custom_call_target="tpu_custom_call" | custom-call | tf_op jit(solution)/shard_map/step/pallas_call | solution.py:513
  73.8 0.6 copy.17

commit v7 on v6

--- a/solution.py
+++ b/solution.py
@@ -86,6 +86,7 @@
     theirs,
     ghost,
     places,
+    columns,
     own,
     force_acc,
     plane_sums,
@@ -300,13 +301,18 @@
         ghost.at[pl.ds(plane, plane)], theirs, ici_send, over_recv, along(0, 0, 1), MESH
     ).start()
     self_sums = [jnp.zeros((1, 128), F32)] * 3
-    columns = jnp.concatenate([ghost[center + q] for q in range(blocks)], axis=0).T
+    def spread_own(first, atoms):
+        for at in range(0, atoms, 8):
+            spot = pl.multiple_of(first + at, 8)
+            column = columns[pl.ds(spot, 8), :]
+            for k in range(8):
+                own[k, pl.ds(spot, 8), :] = jnp.broadcast_to(column[:, k : k + 1], (8, 128))
+
+    for q in range(blocks):
+        columns[q * 128 : q * 128 + 128, :] = ghost[center + q].T
+    spread_own(0, CHUNK)
     for q in range(blocks):
         tile = ghost[center + q]
-        for k in range(8):
-            own[k, q * 128 : q * 128 + 128, :] = jnp.broadcast_to(
-                columns[:, 8 * q + k : 8 * q + k + 1], (128, 128)
-            )
         atom = [tile[r : r + 1] for r in range(8)]
         _, _, _, _, u, root, t, ty, coul = pair(atom, atom)
         v = (ty - t) + coul
@@ -329,6 +335,8 @@
 
         def step(k, sums):
             q = k // (128 // chunk)
+            if with_energy:
+                spread_own(jnp.minimum((k + 1) * chunk, blocks * 128 - WIDE), WIDE)
             atoms = [
                 [own[r, pl.ds(k * chunk + 8 * half, 8), :] for r in range(8)]
                 for half in range(halves)
@@ -533,6 +541,7 @@
             pltpu.VMEM((9 * blocks, 8, 128), F32),
             pltpu.VMEM((27 * blocks + 1, 8, 128), F32),
             pltpu.SMEM((blocks * neighbours.shape[-1],), jnp.int32),
+            pltpu.VMEM((atoms, 8), F32),
             pltpu.VMEM((8, atoms, 128), F32),
             pltpu.VMEM((3, atoms, 128), F32),
             pltpu.VMEM((n_dy * n_dz, 1, 128), F32),

time: 78.1 us -> 81.5 us (1.044)
  Pallas kernels: 72.5 us -> 76 us
    pallas_call x1, Pallas kernels: 72.5 us -> 76 us  [on_device(): pl.pallas_call(lambda *refs: kernel(sizes, *refs), out_shape=(pltpu.VMEM(...]
where the time goes in v7:
time: 81.5 us; the launch traced here: 81.3 us
  Pallas kernels  76 us (93%)
  between operations  4.74 us (6%)
    pallas_call x1, Pallas kernels, on_device(): pl.pallas_call(lambda *refs: kernel(sizes, *refs), out_shape=(pltpu.VMEM(...  76 us

profile of v7, /device:TPU:33, one launch (start us, length us, event | category | flops | bytes accessed | tf_op | source)
XLA Modules:
  0.0 81.3 jit_solution(13129318909698639456)
XLA Ops:
  1.3 76.0 %step.1 = (f32[3,1,1,1,768]{4,3,2,1,0:T(1,128)S(1)}, f32[1]{0:T(128)}, f32[1]{0:T(128)}) custom-call(f32[3,1,1,1,768]{4,3,2,1,0:T(1,128)} %refs_0_.1, s32[1,1,1,768]{3,2,1,0:T(1,128)} %refs_1_.1, s32[1,1,1,768]{3,2,1,0:T(1,128)} %refs_2_.1, s32[1,1,1,2,16]{4,3,2,1,0:T(2,128)} %refs_3_.1, s32[1,1,6,1,16]{4,3,2,1,0:T(1,128)} %bitcast.1, ...), custom_call_target="tpu_custom_call" | custom-call | tf_op jit(solution)/shard_map/step/pallas_call | solution.py:521
  77.2 0.6 copy.17
